TPU v7x, 128 devices: a whole 4x4x4 slice. The times are simulated.
128 devices in a mesh: img: 32 (over y, z, core), grp: 4 (over x).
Axes of the slice: x: 4, y: 4, z: 4, core: 2. Of those that a mesh axis runs over, the one named last changes fastest.
Arguments:
- images: bfloat16 [49152, 9216], P(('img', 'grp')), may hold values from -64 to 64, as said below
- expansion_basis: bfloat16 [9216, 960], P(None, 'img'), may hold values from -0.0625 to 0.0625
- block_sizes: int32 [16], replicated, may hold values from 1 to 80, 480 in all
- keep_count: int32 [16], replicated, may hold values from 1 to 8
- start_block: float32 [16, 80, 8], replicated, may hold values from -6 to 6
Outputs:
- features: float32 [49152, 256], P(('img', 'grp'))
- values: float32 [16, 8], replicated
Inputs may be any that keep to these rules, and one draw needn't show every extreme that they name: `images`: pixel values of order one. `block_sizes`: the 16 sizes sum to 480.
All inputs are finite; a program needn't handle non-finite values.
Results may differ from a plain program's by a relative error of at most 0.025.
Values may be sent and summed in bfloat16 or wider, within the bound.
A program may use at most 128 MiB of HBM per device.

v0:
```python
import jax
import jax.numpy as jnp
from jax import lax
from jax.sharding import Mesh
from jax.sharding import PartitionSpec as P

NMAX = 80
L = 16
S = 480
KMAX = 8
ITERS = 3
IMG = ("img_0", "img_1", "img_2")
IMG_GRP = ("img_0", "img_1", "img_2", "grp")


HIGH = lax.Precision.HIGHEST


def cut_along(shard, dim, peers):
    shape = shard.shape
    tiles = shard.reshape(*shape[:dim], peers, shape[dim] // peers, *shape[dim + 1 :])
    return jnp.moveaxis(tiles, dim, 0)


def sum_at_owner(shard, axis, dim):
    peers = lax.axis_size(axis)
    tiles = lax.all_to_all(cut_along(shard, dim, peers), axis, 0, 0, tiled=True)
    return jnp.sum(tiles, axis=0)


def summed_rows(shard, axes, dim):
    far, near = axes
    tiles = cut_along(shard, dim, lax.axis_size(far))
    nearer = sum_at_owner(tiles, near, dim + 1)
    arrived = lax.all_to_all(nearer, far, split_axis=0, concat_axis=0, tiled=True)
    return arrived.sum(axis=0)


def padded_to(lines, peers):
    spare = -len(lines) % peers
    return jnp.pad(lines, [(0, spare)] + [(0, 0)] * (lines.ndim - 1))


def sent_to_all(shard, axis):
    peers = lax.axis_size(axis)
    return lax.all_to_all(
        jnp.broadcast_to(shard[None], (peers, *shard.shape)), axis, 0, 0, tiled=True
    )


def in_order(tiles, dim):
    shape = list(tiles.shape[1:])
    shape[dim] *= tiles.shape[0]
    return jnp.moveaxis(tiles, 0, dim).reshape(shape)


def gather_axes(shard, axes, dim):
    far, near = axes
    leading = sent_to_all(shard, far)
    tiles = jnp.swapaxes(sent_to_all(leading, near), 0, 1)
    return in_order(tiles.reshape(-1, *shard.shape), dim)


def nested_sum(shard, axes):
    lines = shard.reshape(-1, shard.shape[-1])
    own = summed_rows(padded_to(lines, lax.axis_size(axes[0]) * lax.axis_size(axes[1])), axes, 0)
    whole = gather_axes(own, axes, 0)
    return whole[: len(lines)].reshape(shard.shape)


def selector(block_sizes, total, count, width):
    offsets = jnp.cumsum(block_sizes) - block_sizes
    column = jnp.arange(total, dtype=jnp.int32)[:, None, None]
    inside = jnp.arange(width, dtype=jnp.int32)[None, None, :]
    hit = (column == offsets[None, :, None] + inside) & (inside < block_sizes[None, :, None])
    return hit.astype(jnp.bfloat16).reshape(total, count * width)


def subspace(cover, block_sizes, keep_count, start_block):
    width = cover.shape[1]
    ranks = start_block.shape[2]
    inside = jnp.arange(width, dtype=jnp.int32)[None, :, None] < block_sizes[:, None, None]
    keep = jnp.minimum(keep_count, (block_sizes + 1) // 2)
    current = jnp.where(inside, start_block, jnp.zeros_like(start_block))
    for turn in range(ITERS):
        product = jnp.einsum("bij,bjk->bik", cover, current, precision=HIGH)
        columns = []
        for column_id in range(ranks):
            vector = product[:, :, column_id]
            for earlier in columns:
                vector = vector - jnp.sum(earlier * vector, axis=1, keepdims=True) * earlier
            length = jnp.sqrt(jnp.sum(vector * vector, axis=1, keepdims=True))
            alive = (column_id < keep)[:, None]
            columns.append(jnp.where(alive, vector / length, jnp.zeros_like(vector)))
        current = jnp.stack(columns, axis=2)
    product = jnp.einsum("bij,bjk->bik", cover, current, precision=HIGH)
    found = jnp.sum(current * product, axis=1)
    return (current, found)


def per_device(images, expansion_basis, block_sizes, keep_count, start_block):
    rows = images.shape[0]
    coeffs = jnp.dot(
        images,
        lax.all_gather(expansion_basis, IMG, axis=1, tiled=True),
        preferred_element_type=jnp.float32,
    ).astype(jnp.bfloat16)
    samples = coeffs.reshape(2 * rows, S)
    pick = selector(block_sizes, S, L, NMAX)
    padded = jnp.dot(samples, pick, preferred_element_type=jnp.float32).astype(jnp.bfloat16)
    wide = padded.reshape(2 * rows, L, NMAX)
    scale = 1.0 / (2 * rows * lax.axis_size(IMG) * lax.axis_size("grp"))
    partial_value = (
        jnp.einsum("rli,rlj->lij", wide, wide, preferred_element_type=jnp.float32) * scale
    )
    cover = nested_sum(partial_value, (("img_0", "img_1"), ("img_2", "grp")))
    vectors, found = subspace(cover, block_sizes, keep_count, start_block)
    rounded = vectors.astype(jnp.bfloat16)
    features = jnp.einsum("rli,lij->rlj", wide, rounded, preferred_element_type=jnp.float32)
    return (features.reshape(rows, 2 * L * KMAX), found)


def solution(mesh):
    split = Mesh(
        mesh.devices.reshape(4, 4, 2, mesh.shape["grp"]), ("img_0", "img_1", "img_2", "grp")
    )
    in_specs = (P(IMG_GRP, None), P(None, IMG), P(), P(), P())
    out_specs = (P(IMG_GRP, None), P())
    return jax.shard_map(
        per_device, mesh=split, in_specs=in_specs, out_specs=out_specs, check_vma=False
    )
```

profile of v0, /device:TPU:1, one launch (start us, length us, event | category | flops | bytes accessed | tf_op | source)
XLA Modules:
  0.0 224.9 jit_solution(15298328586002970351)
XLA Ops:
  7.9 0.7 copy.372
  9.4 0.8 broadcast_reduce_fusion
  10.5 80.9 %all-gather.3.cloned.1.call-done = bf16[32,30,9216]{2,1,0:T(8,128)(2,1)} async-done(((bf16[1,30,9216]{2,1,0:T(8,128)(2,1)}), bf16[32,30,9216]{2,1,0:T(8,128)(2,1)}) %all-gather.3.cloned.1.call-update) | async-done | bytes 17694736 | tf_op jit(solution)/shard_map/all_gather | solution.py:105
  91.4 16.4 %reshape.2849 = bf16[960,9216]{1,0:T(8,128)(2,1)} reshape(bf16[32,30,9216]{2,1,0:T(8,128)(2,1)} %all-gather.3.cloned.1.call-done) | data formatting | bytes 35389440
  107.8 15.0 %convolution_convert_fusion.1 = bf16[384,960]{0,1:T(8,128)(2,1)S(1)} fusion(bf16[384,9216]{1,0:T(8,128)(2,1)} %param.5, bf16[960,9216]{1,0:T(8,128)(2,1)} %reshape.2849), kind=kOutput, calls=%fused_computation.3 | convolution fusion | flops 6795141120 | bytes 25509888 | tf_op jit(solution)/shard_map/dot_general | solution.py:103
  123.6 2.5 %convolution_convert_fusion = bf16[768,1280]{1,0:T(8,128)(2,1)} fusion(bf16[768,480]{1,0:T(8,128)(2,1)S(1)} %reshape.2843, s32[1280]{0:T(1024)S(1)} %add.35, pred[1280]{0:T(1024)(128)(4,1)S(1)} %lt.38), kind=kOutput, calls=%fused_computation | convolution fusion | flops 945930240 | bytes 2709760 | tf_op jit(solution)/shard_map/dot_general | solution.py:110
  126.2 2.7 %copy.373 = bf16[768,1280]{0,1:T(8,128)(2,1)S(1)} copy(bf16[768,1280]{1,0:T(8,128)(2,1)} %convolution_convert_fusion) | data formatting | bytes 3932160 | tf_op jit(solution)/shard_map/convert_element_type | solution.py:110
  129.7 15.1 %all_to_all.20 = f32[8,16,10,80]{3,1,2,0:T(8,128)S(1)} all-to-all(f32[8,16,10,80]{3,1,2,0:T(8,128)S(1)} %bitcast.97), channel_id=1, replica_groups=mesh['img_0'=4,'img_1'=4,'img_2'=2,'grp'=4] {'img_2','grp'}, dimensions={0} | all-to-all | bytes 819200 | tf_op jit(solution)/shard_map/all_to_all | solution.py:27
  145.1 11.1 %all_to_all.21 = f32[16,1,800]{2,1,0:T(1,128)S(1)} all-to-all(f32[16,1,800]{2,1,0:T(1,128)S(1)} %reshape.2863), channel_id=1, replica_groups=mesh['img_0'=4,'img_1'=4,'img_2'=2,'grp'=4] {'img_0','img_1'}, dimensions={0} | all-to-all | bytes 102400 | tf_op jit(solution)/shard_map/all_to_all | solution.py:35
  156.7 0.8 reduce.9
  157.7 0.8 reshape.2865
  158.4 3.5 %all-to-all-start.2 = ((f32[16,1,800]{2,1,0:T(1,128)}), f32[16,1,800]{2,1,0:T(1,128)S(1)}, u32[]{:S(2)}, u32[]{:S(2)}) async-start(f32[16,1,800]{2,1,0:T(1,128)} %reshape.2865), calls=%async_computation.2 | async-start | bytes 114688 | tf_op jit(solution)/shard_map/all_to_all | solution.py:46
  162.0 6.4 %all-to-all-done.2 = f32[16,1,800]{2,1,0:T(1,128)S(1)} async-done(((f32[16,1,800]{2,1,0:T(1,128)}), f32[16,1,800]{2,1,0:T(1,128)S(1)}, u32[]{:S(2)}, u32[]{:S(2)}) %all-to-all-start.2) | async-done | bytes 51232 | tf_op jit(solution)/shard_map/all_to_all | solution.py:46
  168.4 0.8 reduce.10
  169.3 0.9 broadcast_in_dim.121
  170.2 6.4 %all-to-all-start.3 = ((f32[8,16,10,80]{3,1,2,0:T(8,128)}), f32[8,16,10,80]{3,1,2,0:T(8,128)S(1)}, u32[]{:S(2)}, u32[]{:S(2)}) async-start(f32[8,16,10,80]{3,1,2,0:T(8,128)} %broadcast_in_dim.121), calls=%async_computation.3 | async-start | bytes 1310720 | tf_op jit(solution)/shard_map/all_to_all | solution.py:46
  176.7 10.7 %all-to-all-done.3 = f32[8,16,10,80]{3,1,2,0:T(8,128)S(1)} async-done(((f32[8,16,10,80]{3,1,2,0:T(8,128)}), f32[8,16,10,80]{3,1,2,0:T(8,128)S(1)}, u32[]{:S(2)}, u32[]{:S(2)}) %all-to-all-start.3) | async-done | bytes 409632 | tf_op jit(solution)/shard_map/all_to_all | solution.py:46
  187.4 1.3 fusion.6
  193.1 1.3 fusion.8
  198.8 1.3 fusion.10
  204.6 1.3 fusion.4
  205.9 0.7 fusion.12
  206.9 4.9 %copy.407 = f32[768,16,8]{2,1,0:T(8,128)} copy(f32[768,16,8]{0,2,1:T(8,128)S(1)} %convolution_bitcast_fusion) | data formatting | bytes 786432 | tf_op jit(solution)/shard_map/rli,lij->rlj/transpose | solution.py:119
  211.8 6.3 %reshape.2847 = f32[384,256]{1,0:T(8,128)} reshape(f32[768,16,8]{2,1,0:T(8,128)} %copy.407) | data formatting | bytes 786432 | tf_op jit(solution)/shard_map/reshape | solution.py:120
  (130 shorter events, 17.9 us)
Async XLA Ops:
  7.2 84.2 %all-gather.3.cloned.1.call-start = ((), (), s32[]{:S(2)}) async-start(), calls=%async_computation.4 | async-start | bytes 19464192 | tf_op jit(solution)/shard_map/all_gather | solution.py:105
  129.5 32.4 %copy-start.1 = (s32[16]{0:T(128)S(1)}, s32[16]{0:T(128)}, u32[]{:S(2)}) copy-start(s32[16]{0:T(128)} %param.7) | copy-start | bytes 196
  144.8 31.8 %copy-start.2 = (s32[16]{0:T(128)S(1)}, s32[16]{0:T(128)}, u32[]{:S(2)}) copy-start(s32[16]{0:T(128)} %param.8) | copy-start | bytes 196
  144.8 42.6 %copy-start = (f32[16,80,8]{1,2,0:T(8,128)S(1)}, f32[16,80,8]{1,2,0:T(8,128)}, u32[]{:S(2)}) copy-start(f32[16,80,8]{1,2,0:T(8,128)} %param.9) | copy-start | bytes 122884
  158.4 10.0 %all-to-all-start.2 = ((f32[16,1,800]{2,1,0:T(1,128)}), f32[16,1,800]{2,1,0:T(1,128)S(1)}, u32[]{:S(2)}, u32[]{:S(2)}) async-start(f32[16,1,800]{2,1,0:T(1,128)} %reshape.2865), calls=%async_computation.2 | async-start | bytes 114688 | tf_op jit(solution)/shard_map/all_to_all | solution.py:46
  170.2 17.2 %all-to-all-start.3 = ((f32[8,16,10,80]{3,1,2,0:T(8,128)}), f32[8,16,10,80]{3,1,2,0:T(8,128)S(1)}, u32[]{:S(2)}, u32[]{:S(2)}) async-start(f32[8,16,10,80]{3,1,2,0:T(8,128)} %broadcast_in_dim.121), calls=%async_computation.3 | async-start | bytes 1310720 | tf_op jit(solution)/shard_map/all_to_all | solution.py:46
Sparse Core Ops, SparseCore 0:
  10.2 81.1 all-gather.2
where the time goes:
time: 226 us; the launch traced here: 225 us
  waiting for transfers between devices  98.7 us (44%)
  local copies, waits for them, and re-layouts  35.9 us (16%)
  blocking collectives  26.2 us (12%)
  matrix products  23.7 us (10%)
  other arithmetic  15.9 us (7%)
  between operations  14.5 us (6%)
  starting transfers between devices  9.98 us (4%)
    all_gather x1, waiting for transfers between devices, per_device(): lax.all_gather(expansion_basis, IMG, axis=1, tiled=True)  80.9 us
    unnamed x11, local copies, waits for them, and re-layouts  17.5 us
    all_to_all x2, waiting for transfers between devices, sent_to_all(): lax.all_to_all(jnp.broadcast_to(shard[None], (peers, *shard.shape)), axis...  17.1 us
    all_to_all x1, blocking collectives, sum_at_owner(): tiles = lax.all_to_all(cut_along(shard, dim, peers), axis, 0, 0, tiled=True)  15.1 us
    dot_general x1, matrix products, per_device(): jnp.dot(images, lax.all_gather(expansion_basis, IMG, axis=1, tiled=True),...  15 us
    all_to_all x1, blocking collectives, summed_rows(): lax.all_to_all(nearer, far, split_axis=0, concat_axis=0, tiled=True)  11.1 us
    all_to_all x2, starting transfers between devices, sent_to_all(): lax.all_to_all(jnp.broadcast_to(shard[None], (peers, *shard.shape)), axis...  9.94 us
    reduce_sum x30, other arithmetic, subspace(): vector = vector - jnp.sum(earlier * vector, axis=1, keepdims=True) * earlier  6.8 us
  transfers between devices with their start and end apart: 3, of which 3 were waited for; matrix products, arithmetic and copies ran while one was open for 1% of the time, Pallas kernels for 0%

commit v1 on v0

--- a/solution.py
+++ b/solution.py
@@ -1,6 +1,11 @@
+import functools
+import heapq
+
 import jax
 import jax.numpy as jnp
 from jax import lax
+from jax.experimental import pallas as pl
+from jax.experimental.pallas import tpu as pltpu
 from jax.sharding import Mesh
 from jax.sharding import PartitionSpec as P
 
@@ -9,11 +14,225 @@
 S = 480
 KMAX = 8
 ITERS = 3
-IMG = ("img_0", "img_1", "img_2")
-IMG_GRP = ("img_0", "img_1", "img_2", "grp")
-
-
+AXES = ("img_0", "img_1", "img_2", "grp")
+IMG = AXES[:3]
+IMG_GRP = AXES
 HIGH = lax.Precision.HIGHEST
+MESH = pl.DeviceIdType.MESH
+
+KC = 256
+SUBS = 4
+ROUNDS = 6
+CHUNKS = 16 + (ROUNDS - 1) * SUBS
+ROWS = 32
+BLOCK = ROWS * KC * 2
+
+
+class Plan:
+    def __init__(self, ahead=2, rate=44e3, hop=1.9, d_rate=500e3, d_hop=1.1, dot=0.3):
+        self.program = []
+        self.sems = {}
+        busy = {}
+        now = 0.0
+        heap = []
+        arrived = {}
+        ready = []
+
+        def send(key, link, size):
+            sem = self.sems.setdefault(key, len(self.sems))
+            fast = link == "d"
+            begin = max(busy.get(link, 0.0), now)
+            end = begin + size / (d_rate if fast else rate)
+            busy[link] = end
+            heapq.heappush(heap, (end + (d_hop if fast else hop), sem, key))
+            self.program.append(("send", key))
+
+        def axes(sub):
+            return ("y", "z") if sub < 2 else ("z", "y")
+
+        def way(sub):
+            return ("+", "-") if sub % 2 == 0 else ("-", "+")
+
+        def start_round(r):
+            for sub in range(SUBS):
+                a = axes(sub)[0]
+                send(("1", r, sub, 0), a + "+", BLOCK)
+                send(("1", r, sub, 1), a + "-", BLOCK)
+
+        def spread(kind, rest, axis, sub, size):
+            send((kind, *rest, 0), axis + "+", size)
+            send((kind, *rest, 1), axis + "-", size)
+
+        def got(group, need):
+            arrived[group] = arrived.get(group, 0) + 1
+            return arrived[group] == need
+
+        def half_done(chunk):
+            send(("D", chunk), "d", 16 * BLOCK)
+            if got(("C", chunk), 2):
+                ready.append(chunk)
+
+        started = 0
+        while started < min(ahead, ROUNDS):
+            start_round(started)
+            started += 1
+        while heap or ready:
+            if ready and (not heap or heap[0][0] > now or len(ready) > 3):
+                chunk = ready.pop(0)
+                self.program.append(("dot", chunk))
+                now += dot
+                continue
+            when, _, key = heapq.heappop(heap)
+            now = max(now, when) + 0.02
+            self.program.append(("wait", key))
+            kind = key[0]
+            if kind in ("1", "2"):
+                _, r, sub, j = key
+                axis = axes(sub)[0 if kind == "1" else 1]
+                size = BLOCK if kind == "1" else 4 * BLOCK
+                if j == sub % 2:
+                    send((kind, r, sub, 2), axis + way(sub)[0], size)
+                if kind == "1" and got(("1", r, sub), 3):
+                    spread("2", (r, sub), axes(sub)[1], sub, 4 * BLOCK)
+                    if r == 0:
+                        spread("X", (sub, 0), "x", sub, 4 * BLOCK)
+                    if sub == SUBS - 1 and started < ROUNDS:
+                        start_round(started)
+                        started += 1
+                if kind == "2":
+                    if r == 0:
+                        spread("X", (sub, 1 + j), "x", sub, 4 * BLOCK)
+                    if got(("2", r, sub), 3):
+                        half_done(("own", sub) if r == 0 else ("all", r, sub))
+            elif kind == "X":
+                _, sub, piece, j = key
+                if j == sub % 2:
+                    send(("X", sub, piece, 2), "x" + way(sub)[0], 4 * BLOCK)
+                if got(("X", sub, j), 4):
+                    half_done(("far", j, sub))
+            else:
+                if got(("C", key[1]), 2):
+                    ready.append(key[1])
+        self.end = now
+
+
+def gather_dot(plan, images, own, coeffs, held, pixels, total, fill_sem, send_sem, recv_sem):
+    y, z, c, x = (lax.axis_index(a) for a in AXES)
+
+    def turn(v, by):
+        return lax.rem(v + (by + 4), 4)
+
+    def device(axis, by):
+        spot = {"y": y, "z": z, "x": x}
+        spot[axis] = turn(spot[axis], by)
+        return (spot["y"], spot["z"], c, spot["x"])
+
+    sibling = (y, z, 1 - c, x)
+    barrier = pltpu.get_barrier_semaphore()
+    fills = [
+        pltpu.make_async_copy(own.at[pl.ds(4 * x, 4)], held.at[pl.ds(4 * x, 4), y, z, c], fill_sem.at[0]),
+        pltpu.make_async_copy(own.at[pl.ds(16, CHUNKS - 16)], held.at[pl.ds(16, CHUNKS - 16), y, z, c], fill_sem.at[1]),
+        pltpu.make_async_copy(images, pixels, fill_sem.at[2]),
+    ]
+    for fill in fills:
+        fill.start()
+    for axis in "yzx":
+        for by in (1, -1):
+            pl.semaphore_signal(barrier, inc=1, device_id=device(axis, by), device_id_type=MESH)
+    pl.semaphore_signal(barrier, inc=1, device_id=sibling, device_id_type=MESH)
+    total[...] = jnp.zeros_like(total)
+    pl.semaphore_wait(barrier, 7)
+    fills[0].wait()
+    fills[1].wait()
+
+    SHIFT = (-1, 1, 2)
+
+    def index(chunk):
+        if chunk[0] == "own":
+            return 4 * x + chunk[1]
+        if chunk[0] == "far":
+            return 4 * turn(x, SHIFT[chunk[1]]) + chunk[2]
+        return 16 + (chunk[1] - 1) * SUBS + chunk[2]
+
+    def copy_of(key):
+        kind = key[0]
+        if kind == "D":
+            part = held.at[index(key[1]), :, :, c]
+            where = sibling
+        else:
+            j = key[-1]
+            sub = key[2] if kind != "X" else key[1]
+            step = (1, -1)[j] if j < 2 else (1, -1)[sub % 2]
+            back = 0 if j < 2 else -step
+            first = sub < 2
+            if kind == "1":
+                k = index(("own", sub) if key[1] == 0 else ("all", key[1], sub))
+                part = held.at[k, turn(y, back), z, c] if first else held.at[k, y, turn(z, back), c]
+                where = device("y" if first else "z", step)
+            elif kind == "2":
+                k = index(("own", sub) if key[1] == 0 else ("all", key[1], sub))
+                part = held.at[k, :, turn(z, back), c] if first else held.at[k, turn(y, back), :, c]
+                where = device("z" if first else "y", step)
+            else:
+                k = 4 * turn(x, back) + sub
+                shift = (0, *SHIFT)[key[2]]
+                if key[2] == 3:
+                    shift = 2
+                part = held.at[k, :, turn(z, shift), c] if first else held.at[k, turn(y, shift), :, c]
+                where = device("x", step)
+        sem = plan.sems[key]
+        return pltpu.make_async_remote_copy(
+            src_ref=part, dst_ref=part, send_sem=send_sem, recv_sem=recv_sem.at[sem],
+            device_id=where, device_id_type=MESH,
+        )
+
+    sent = []
+    loaded = False
+    for op, what in plan.program:
+        if op == "send":
+            copy = copy_of(what)
+            copy.start()
+            sent.append(copy)
+        elif op == "wait":
+            copy_of(what).wait_recv()
+        else:
+            if not loaded:
+                fills[2].wait()
+                loaded = True
+            k = index(what)
+            block = held[k].reshape(32 * ROWS, KC)
+            rows = pixels[:, pl.ds(pl.multiple_of(k * KC, KC), KC)]
+            total[...] += lax.dot_general(
+                rows, block, (((1,), (1,)), ((), ())), preferred_element_type=jnp.float32
+            )
+    for copy in sent:
+        copy.wait_send()
+    coeffs[...] = total[...].astype(coeffs.dtype)
+
+
+def gathered_coeffs(images, basis):
+    plan = Plan()
+    rows = images.shape[0]
+    own = jnp.pad(basis.T, ((0, ROWS - basis.shape[1]), (0, 0)))
+    own = own.reshape(ROWS, CHUNKS, KC).swapaxes(0, 1)
+    any_ = pl.BlockSpec(memory_space=pl.ANY)
+    return pl.pallas_call(
+        functools.partial(gather_dot, plan),
+        out_shape=jax.ShapeDtypeStruct((rows, 32 * ROWS), jnp.bfloat16),
+        in_specs=[any_, any_],
+        out_specs=pl.BlockSpec(memory_space=pltpu.VMEM),
+        scratch_shapes=[
+            pltpu.VMEM((CHUNKS, 4, 4, 2, ROWS, KC), jnp.bfloat16),
+            pltpu.VMEM(images.shape, jnp.bfloat16),
+            pltpu.VMEM((rows, 32 * ROWS), jnp.float32),
+            pltpu.SemaphoreType.DMA((3,)),
+            pltpu.SemaphoreType.DMA,
+            pltpu.SemaphoreType.DMA((len(plan.sems),)),
+        ],
+        compiler_params=pltpu.CompilerParams(
+            collective_id=0, has_side_effects=True, vmem_limit_bytes=48 * 1024 * 1024
+        ),
+    )(images, own)
 
 
 def cut_along(shard, dim, peers):
@@ -68,12 +287,13 @@
     return whole[: len(lines)].reshape(shard.shape)
 
 
-def selector(block_sizes, total, count, width):
+def selector(block_sizes, count, width):
     offsets = jnp.cumsum(block_sizes) - block_sizes
-    column = jnp.arange(total, dtype=jnp.int32)[:, None, None]
+    place = jnp.arange(16 * ROWS, dtype=jnp.int32)
+    column = jnp.where(place % ROWS < 30, place // ROWS * 30 + place % ROWS, -1)[:, None, None]
     inside = jnp.arange(width, dtype=jnp.int32)[None, None, :]
     hit = (column == offsets[None, :, None] + inside) & (inside < block_sizes[None, :, None])
-    return hit.astype(jnp.bfloat16).reshape(total, count * width)
+    return hit.astype(jnp.bfloat16).reshape(16 * ROWS, count * width)
 
 
 def subspace(cover, block_sizes, keep_count, start_block):
@@ -100,13 +320,9 @@
 
 def per_device(images, expansion_basis, block_sizes, keep_count, start_block):
     rows = images.shape[0]
-    coeffs = jnp.dot(
-        images,
-        lax.all_gather(expansion_basis, IMG, axis=1, tiled=True),
-        preferred_element_type=jnp.float32,
-    ).astype(jnp.bfloat16)
-    samples = coeffs.reshape(2 * rows, S)
-    pick = selector(block_sizes, S, L, NMAX)
+    coeffs = gathered_coeffs(images, expansion_basis)
+    samples = coeffs.reshape(2 * rows, 16 * ROWS)
+    pick = selector(block_sizes, L, NMAX)
     padded = jnp.dot(samples, pick, preferred_element_type=jnp.float32).astype(jnp.bfloat16)
     wide = padded.reshape(2 * rows, L, NMAX)
     scale = 1.0 / (2 * rows * lax.axis_size(IMG) * lax.axis_size("grp"))

time: 226 us -> 153 us (0.68)
  waiting for transfers between devices: 98.7 us -> 17.1 us
  Pallas kernels: 0 us -> 54.2 us
  local copies, waits for them, and re-layouts: 35.9 us -> 20.2 us
  matrix products: 23.7 us -> 8.76 us
  between operations: 14.5 us -> 1.12 us
    all_gather x1 -> x0, waiting for transfers between devices: 80.9 us -> none  [per_device(): lax.all_gather(expansion_basis, IMG, axis=1, tiled=True)]
    pallas_call x0 -> x1, Pallas kernels: none -> 54.2 us  [gathered_coeffs(): pl.pallas_call(functools.partial(gather_dot, plan), out_shape=jax.ShapeDt...]
    unnamed x11 -> x10, local copies, waits for them, and re-layouts: 17.5 us -> 1.12 us
    dot_general x1 -> x0, matrix products: 15 us -> none  [per_device(): jnp.dot(images, lax.all_gather(expansion_basis, IMG, axis=1, tiled=True),...]
  transfers between devices with their start and end apart: 3 -> 2, of which waited for: 3 -> 2; matrix products, arithmetic and copies ran while one was open for 1% -> 0% of each run, Pallas kernels for 0% -> 0%
where the time goes in v1:
time: 153 us; the launch traced here: 152 us
  Pallas kernels  54.2 us (35%)
  blocking collectives  25 us (16%)
  local copies, waits for them, and re-layouts  20.2 us (13%)
  waiting for transfers between devices  17.1 us (11%)
  other arithmetic  15.9 us (10%)
  starting transfers between devices  9.94 us (6%)
  matrix products  8.76 us (6%)
    pallas_call x1, Pallas kernels, gathered_coeffs(): pl.pallas_call(functools.partial(gather_dot, plan), out_shape=jax.ShapeDt...  54.2 us
    all_to_all x2, waiting for transfers between devices, sent_to_all(): lax.all_to_all(jnp.broadcast_to(shard[None], (peers, *shard.shape)), axis...  17.1 us
    all_to_all x1, blocking collectives, sum_at_owner(): tiles = lax.all_to_all(cut_along(shard, dim, peers), axis, 0, 0, tiled=True)  13.6 us
    all_to_all x1, blocking collectives, summed_rows(): lax.all_to_all(nearer, far, split_axis=0, concat_axis=0, tiled=True)  11.3 us
    all_to_all x2, starting transfers between devices, sent_to_all(): lax.all_to_all(jnp.broadcast_to(shard[None], (peers, *shard.shape)), axis...  9.94 us
    reduce_sum x30, other arithmetic, subspace(): vector = vector - jnp.sum(earlier * vector, axis=1, keepdims=True) * earlier  6.8 us
    reshape x1, local copies, waits for them, and re-layouts, per_device(): return (features.reshape(rows, 2 * L * KMAX), found)  6.31 us
    dot_general x4, matrix products, subspace(): product = jnp.einsum('bij,bjk->bik', cover, current, precision=HIGH)  5.13 us
  transfers between devices with their start and end apart: 2, of which 2 were waited for; matrix products, arithmetic and copies ran while one was open for 0% of the time, Pallas kernels for 0%

profile of v1, /device:TPU:1, one launch (start us, length us, event | category | flops | bytes accessed | tf_op | source)
XLA Modules:
  0.0 152.2 jit_solution(11989198409047548318)
XLA Ops:
  0.6 0.7 copy.372
  2.3 0.8 broadcast_reduce_fusion
  3.2 1.1 pad.4
  4.4 54.2 %shard_map.68 = bf16[384,1024]{1,0:T(8,128)(2,1)S(1)} custom-call(bf16[384,9216]{1,0:T(8,128)(2,1)} %images.1, bf16[36,32,256]{2,1,0:T(8,128)(2,1)S(1)} %bitcast.94), custom_call_target="tpu_custom_call" | custom-call | tf_op jit(solution)/shard_map/pallas_call | solution.py:219
  58.9 2.6 %convolution_convert_fusion = bf16[768,1280]{1,0:T(8,128)(2,1)} fusion(bf16[768,512]{1,0:T(8,128)(2,1)S(1)} %reshape.2871, s32[1280]{0:T(1024)S(1)} %add.63, s32[512]{0:T(512)S(1)} %fusion.27, pred[1280]{0:T(1024)(128)(4,1)S(1)} %lt.55), kind=kOutput, calls=%fused_computation | convolution fusion | flops 1008926720 | bytes 2760960 | tf_op jit(solution)/shard_map/dot_general | solution.py:326
  61.5 2.7 %copy.373 = bf16[768,1280]{0,1:T(8,128)(2,1)S(1)} copy(bf16[768,1280]{1,0:T(8,128)(2,1)} %convolution_convert_fusion) | data formatting | bytes 3932160 | tf_op jit(solution)/shard_map/convert_element_type | solution.py:326
  64.2 0.7 convolution_multiply_fusion
  65.1 13.6 %all_to_all.20 = f32[8,16,10,80]{3,1,2,0:T(8,128)S(1)} all-to-all(f32[8,16,10,80]{3,1,2,0:T(8,128)S(1)} %bitcast.101), channel_id=1, replica_groups=mesh['img_0'=4,'img_1'=4,'img_2'=2,'grp'=4] {'img_2','grp'}, dimensions={0} | all-to-all | bytes 819200 | tf_op jit(solution)/shard_map/all_to_all | solution.py:246
  79.0 11.3 %all_to_all.21 = f32[16,1,800]{2,1,0:T(1,128)S(1)} all-to-all(f32[16,1,800]{2,1,0:T(1,128)S(1)} %reshape.2889), channel_id=1, replica_groups=mesh['img_0'=4,'img_1'=4,'img_2'=2,'grp'=4] {'img_0','img_1'}, dimensions={0} | all-to-all | bytes 102400 | tf_op jit(solution)/shard_map/all_to_all | solution.py:254
  90.8 0.8 reduce.9
  91.8 0.8 reshape.2891
  92.5 3.5 %all-to-all-start.2 = ((f32[16,1,800]{2,1,0:T(1,128)}), f32[16,1,800]{2,1,0:T(1,128)S(1)}, u32[]{:S(2)}, u32[]{:S(2)}) async-start(f32[16,1,800]{2,1,0:T(1,128)} %reshape.2891), calls=%async_computation.2 | async-start | bytes 114688 | tf_op jit(solution)/shard_map/all_to_all | solution.py:265
  96.1 6.4 %all-to-all-done.2 = f32[16,1,800]{2,1,0:T(1,128)S(1)} async-done(((f32[16,1,800]{2,1,0:T(1,128)}), f32[16,1,800]{2,1,0:T(1,128)S(1)}, u32[]{:S(2)}, u32[]{:S(2)}) %all-to-all-start.2) | async-done | bytes 51232 | tf_op jit(solution)/shard_map/all_to_all | solution.py:265
  102.5 0.8 reduce.10
  103.4 0.9 broadcast_in_dim.123
  104.3 6.4 %all-to-all-start.3 = ((f32[8,16,10,80]{3,1,2,0:T(8,128)}), f32[8,16,10,80]{3,1,2,0:T(8,128)S(1)}, u32[]{:S(2)}, u32[]{:S(2)}) async-start(f32[8,16,10,80]{3,1,2,0:T(8,128)} %broadcast_in_dim.123), calls=%async_computation.3 | async-start | bytes 1310720 | tf_op jit(solution)/shard_map/all_to_all | solution.py:265
  110.8 10.7 %all-to-all-done.3 = f32[8,16,10,80]{3,1,2,0:T(8,128)S(1)} async-done(((f32[8,16,10,80]{3,1,2,0:T(8,128)}), f32[8,16,10,80]{3,1,2,0:T(8,128)S(1)}, u32[]{:S(2)}, u32[]{:S(2)}) %all-to-all-start.3) | async-done | bytes 409632 | tf_op jit(solution)/shard_map/all_to_all | solution.py:265
  121.5 1.3 fusion.7
  127.2 1.3 fusion.9
  132.9 1.3 fusion.11
  138.7 1.3 fusion.5
  140.0 0.7 fusion.13
  141.0 4.9 %copy.407 = f32[768,16,8]{2,1,0:T(8,128)} copy(f32[768,16,8]{0,2,1:T(8,128)S(1)} %convolution_bitcast_fusion) | data formatting | bytes 786432 | tf_op jit(solution)/shard_map/rli,lij->rlj/transpose | solution.py:335
  145.9 6.3 %reshape.2875 = f32[384,256]{1,0:T(8,128)} reshape(f32[768,16,8]{2,1,0:T(8,128)} %copy.407) | data formatting | bytes 786432 | tf_op jit(solution)/shard_map/reshape | solution.py:336
  (128 shorter events, 16.1 us)
Async XLA Ops:
  65.0 31.0 %copy-start.1 = (s32[16]{0:T(128)S(1)}, s32[16]{0:T(128)}, u32[]{:S(2)}) copy-start(s32[16]{0:T(128)} %param.7) | copy-start | bytes 196
  78.8 32.0 %copy-start.2 = (s32[16]{0:T(128)S(1)}, s32[16]{0:T(128)}, u32[]{:S(2)}) copy-start(s32[16]{0:T(128)} %param.8) | copy-start | bytes 196
  78.8 42.7 %copy-start = (f32[16,80,8]{1,2,0:T(8,128)S(1)}, f32[16,80,8]{1,2,0:T(8,128)}, u32[]{:S(2)}) copy-start(f32[16,80,8]{1,2,0:T(8,128)} %param.9) | copy-start | bytes 122884
  92.5 10.0 %all-to-all-start.2 = ((f32[16,1,800]{2,1,0:T(1,128)}), f32[16,1,800]{2,1,0:T(1,128)S(1)}, u32[]{:S(2)}, u32[]{:S(2)}) async-start(f32[16,1,800]{2,1,0:T(1,128)} %reshape.2891), calls=%async_computation.2 | async-start | bytes 114688 | tf_op jit(solution)/shard_map/all_to_all | solution.py:265
  104.3 17.2 %all-to-all-start.3 = ((f32[8,16,10,80]{3,1,2,0:T(8,128)}), f32[8,16,10,80]{3,1,2,0:T(8,128)S(1)}, u32[]{:S(2)}, u32[]{:S(2)}) async-start(f32[8,16,10,80]{3,1,2,0:T(8,128)} %broadcast_in_dim.123), calls=%async_computation.3 | async-start | bytes 1310720 | tf_op jit(solution)/shard_map/all_to_all | solution.py:265

commit v2 on v1

--- a/solution.py
+++ b/solution.py
@@ -16,7 +16,6 @@
 ITERS = 3
 AXES = ("img_0", "img_1", "img_2", "grp")
 IMG = AXES[:3]
-IMG_GRP = AXES
 HIGH = lax.Precision.HIGHEST
 MESH = pl.DeviceIdType.MESH
 
@@ -26,6 +25,8 @@
 CHUNKS = 16 + (ROUNDS - 1) * SUBS
 ROWS = 32
 BLOCK = ROWS * KC * 2
+PART = 16 * ROWS
+WIN = 96
 
 
 class Plan:
@@ -116,17 +117,18 @@
         self.end = now
 
 
+def turn(v, by):
+    return lax.rem(v + (by + 4), 4)
+
+
+def device(axis, by):
+    spot = dict(zip("yzcx", (lax.axis_index(a) for a in AXES)))
+    spot[axis] = turn(spot[axis], by)
+    return tuple(spot[a] for a in "yzcx")
+
+
 def gather_dot(plan, images, own, coeffs, held, pixels, total, fill_sem, send_sem, recv_sem):
     y, z, c, x = (lax.axis_index(a) for a in AXES)
-
-    def turn(v, by):
-        return lax.rem(v + (by + 4), 4)
-
-    def device(axis, by):
-        spot = {"y": y, "z": z, "x": x}
-        spot[axis] = turn(spot[axis], by)
-        return (spot["y"], spot["z"], c, spot["x"])
-
     sibling = (y, z, 1 - c, x)
     barrier = pltpu.get_barrier_semaphore()
     fills = [
@@ -136,10 +138,8 @@
     ]
     for fill in fills:
         fill.start()
-    for axis in "yzx":
-        for by in (1, -1):
-            pl.semaphore_signal(barrier, inc=1, device_id=device(axis, by), device_id_type=MESH)
-    pl.semaphore_signal(barrier, inc=1, device_id=sibling, device_id_type=MESH)
+    for peer in [device(axis, by) for axis in "yzx" for by in (1, -1)] + [sibling]:
+        pl.semaphore_signal(barrier, inc=1, device_id=peer, device_id_type=MESH)
     total[...] = jnp.zeros_like(total)
     pl.semaphore_wait(barrier, 7)
     fills[0].wait()
@@ -210,138 +210,245 @@
     coeffs[...] = total[...].astype(coeffs.dtype)
 
 
-def gathered_coeffs(images, basis):
+def places(sizes):
+    offsets, firsts = [], []
+    offset = jnp.int32(0)
+    for l in range(L):
+        offsets.append(offset)
+        place = lax.div(offset, 30) * ROWS + lax.rem(offset, 30)
+        firsts.append(jnp.minimum(lax.div(place, 8) * 8, PART - WIN))
+        offset = offset + sizes[l]
+    return offsets, firsts
+
+
+def cut_windows(sizes, keeps, coeffs, start, packed, begin, gram):
+    def part_gram(p):
+        some = coeffs[:, p * PART : (p + 1) * PART]
+        return lax.dot_general(some, some, (((0,), (0,)), ((), ())), preferred_element_type=jnp.float32)
+
+    gram[...] = part_gram(0) + part_gram(1)
+
+    offsets, firsts = places(sizes)
+
+    def window(l):
+        left = jnp.minimum(lax.div(firsts[l], 128), 2) * 128
+        rows = gram[pl.ds(pl.multiple_of(firsts[l], 8), WIN), pl.ds(pl.multiple_of(left, 128), 256)]
+        return pltpu.roll(rows, lax.rem(256 - (firsts[l] - left), 256), 1)[:, :128]
+
+    lane = lax.broadcasted_iota(jnp.int32, (32, 128), 1)
+    for pair in range(L // 2):
+        one, two = window(2 * pair), window(2 * pair + 1)
+        xo, co = pair // 2, pair % 2
+        packed[xo, co, 0] = jnp.where(lane < 96, one[:32], pltpu.roll(one[64:], 32, 1))
+        packed[xo, co, 1] = jnp.where(lane < 96, two[:32], pltpu.roll(two[64:], 32, 1))
+        packed[xo, co, 2] = jnp.where(lane < 64, pltpu.roll(one[32:64], 96, 1), pltpu.roll(two[32:64], 32, 1))
+
+    row = lax.broadcasted_iota(jnp.int32, (KMAX, 128), 0)
+    place = lax.broadcasted_iota(jnp.int32, (NMAX, 128), 1)
+    inner = lax.broadcasted_iota(jnp.int32, (NMAX, 128), 0)
+    for l in range(L):
+        slot = lax.rem(firsts[l] + place, ROWS)
+        source = lax.div(firsts[l] + place, ROWS) * 30 + slot - offsets[l]
+        source = jnp.where(slot < 30, source, -1)
+        hit = ((source == inner) & (inner < sizes[l])).astype(jnp.float32)
+        lines = slice(KMAX * l, KMAX * l + KMAX)
+        begin[0, lines] = jnp.dot(start[l], hit, precision=HIGH, preferred_element_type=jnp.float32)
+        begin[1, lines] = jnp.broadcast_to(jnp.sum(hit, axis=0, keepdims=True), (KMAX, 128))
+        keep = jnp.minimum(keeps[l], lax.div(sizes[l] + 1, 2))
+        begin[2, lines] = (row < keep).astype(jnp.float32)
+
+
+def iterate(summed, current, inside, alive):
+    wide = lax.broadcasted_iota(jnp.int32, (128, 128), 1)
+    block_row = lax.div(lax.broadcasted_iota(jnp.int32, (128, 128), 0), 32) * 32
+
+    def cover_of(i):
+        low = jnp.zeros((32, 128), jnp.float32)
+        middle = pltpu.roll(summed[2], 32 if i == 0 else 96, 1)
+        upper = jnp.concatenate([summed[i], middle, pltpu.roll(summed[i], 96, 1), low], axis=0)
+        upper = jnp.where((wide >= block_row) & (wide < WIN), upper, 0.0)
+        beyond = jnp.where(wide >= block_row + 32, upper, 0.0)
+        return upper + beyond.T
+
+    row = lax.broadcasted_iota(jnp.int32, (KMAX, 128), 0)
+    column = lax.broadcasted_iota(jnp.int32, (KMAX, 128), 1)
+
+    def times(current, cover):
+        return jnp.dot(current, cover, precision=HIGH, preferred_element_type=jnp.float32)
+
+    covers = [cover_of(i) for i in range(2)]
+    lines = [slice(KMAX * i, KMAX * i + KMAX) for i in range(2)]
+    currents = [current[i] for i in lines]
+    inside = [inside[i] > 0.5 for i in lines]
+    alive = [alive[i] > 0.5 for i in lines]
+    for turn_id in range(ITERS):
+        stacks = [jnp.where(inside[i], times(currents[i], covers[i]), 0.0) for i in range(2)]
+        norms = [jnp.ones((KMAX, 1), jnp.float32) for _ in range(2)]
+        for m in range(KMAX):
+            for i in range(2):
+                vector = stacks[i][m : m + 1]
+                dots = jnp.sum(stacks[i] * vector, axis=1, keepdims=True)
+                square = dots[m : m + 1]
+                norms[i] = jnp.where(row[:, :1] == m, square, norms[i])
+                if m < KMAX - 1:
+                    stacks[i] = jnp.where(row > m, stacks[i] - dots / square * vector, stacks[i])
+        currents = [jnp.where(alive[i], stacks[i] / jnp.sqrt(norms[i]), 0.0) for i in range(2)]
+    ends = []
+    for i in range(2):
+        quotient = jnp.sum(currents[i] * times(currents[i], covers[i]), axis=1, keepdims=True)
+        ends.append(jnp.where(column == 127, quotient, currents[i]))
+    return jnp.concatenate(ends, axis=0)
+
+
+def reduce_iterate(
+    scale, packed, begin, everything, half, mate, by_x, by_y, by_z, found, mate_sem, far_sem, found_sem
+):
+    y, z, c, x = (lax.axis_index(a) for a in AXES)
+    sibling = (y, z, 1 - c, x)
+    owners = [device("x", by) for by in (1, 2, 3)] + [(y, z, 1 - c, turn(x, by)) for by in range(4)]
+    others = [device(axis, by) for axis in "yz" for by in (1, 2, 3)]
+    barrier = pltpu.get_barrier_semaphore()
+    for peer in owners + others:
+        pl.semaphore_signal(barrier, inc=1, device_id=peer, device_id_type=MESH)
+    pl.semaphore_wait(barrier, 13)
+
+    def push(src, dst, send, recv, where):
+        copy = pltpu.make_async_remote_copy(
+            src_ref=src, dst_ref=dst, send_sem=send, recv_sem=recv, device_id=where, device_id_type=MESH
+        )
+        copy.start()
+        return copy
+
+    copy = push(packed.at[:, 1 - c], mate, mate_sem.at[0], mate_sem.at[1], sibling)
+    copy.wait()
+    for xo in range(4):
+        half[xo] = packed[xo, c] + mate[xo]
+    copies = [
+        push(half.at[turn(x, by)], by_x.at[by - 1], far_sem.at[0, by - 1], far_sem.at[1, by - 1], device("x", by))
+        for by in (1, 2, 3)
+    ]
+    for copy in copies:
+        copy.wait()
+    by_y[y] = half[x] + by_x[0] + by_x[1] + by_x[2]
+    copies = [
+        push(by_y.at[y], by_y.at[y], far_sem.at[2, by - 1], far_sem.at[3, by - 1], device("y", by)) for by in (1, 2, 3)
+    ]
+    for copy in copies:
+        copy.wait()
+    by_z[z] = by_y[0] + by_y[1] + by_y[2] + by_y[3]
+    copies = [
+        push(by_z.at[z], by_z.at[z], far_sem.at[4, by - 1], far_sem.at[5, by - 1], device("z", by)) for by in (1, 2, 3)
+    ]
+    for copy in copies:
+        copy.wait()
+    me = 2 * x + c
+    lines = pl.ds(pl.multiple_of(2 * KMAX * me, 2 * KMAX), 2 * KMAX)
+    found[me] = iterate(
+        (by_z[0] + by_z[1] + by_z[2] + by_z[3]) * scale, begin[0, lines], begin[1, lines], begin[2, lines]
+    )
+    copies = [
+        push(found.at[me], found.at[me], found_sem.at[0, e], found_sem.at[1, e], owners[e]) for e in range(7)
+    ]
+    for copy in copies:
+        copy.wait()
+
+    everything[...] = found[...].reshape(L * KMAX, 128)
+
+
+def project(sizes, coeffs, everything, features, values):
+    firsts = places(sizes)[1]
+    tall = lax.broadcasted_iota(jnp.int32, (L * KMAX, 128), 0)
+    wide = lax.broadcasted_iota(jnp.int32, (L * KMAX, 128), 1)
+    spread = jnp.where(lax.rem(tall, KMAX) == wide, everything[:, 127:128], 0.0)
+    choose = lax.div(lax.broadcasted_iota(jnp.int32, (L, 128), 1), KMAX) == lax.broadcasted_iota(jnp.int32, (L, 128), 0)
+    values[...] = jnp.dot(
+        choose.astype(jnp.float32), spread, precision=HIGH, preferred_element_type=jnp.float32
+    )[:, :KMAX]
+    lines = []
+    for l in range(L):
+        line = jnp.where(wide[:KMAX] < WIN, everything[KMAX * l : KMAX * l + KMAX], 0.0)
+        line = jnp.concatenate([line, jnp.zeros((KMAX, PART - 128), jnp.float32)], axis=1)
+        lines.append(pltpu.roll(line, firsts[l], 1))
+    rounded = jnp.concatenate(lines, axis=0).astype(jnp.bfloat16)
+    for p in range(2):
+        features[:, p * 128 : (p + 1) * 128] = lax.dot_general(
+            coeffs[:, p * PART : (p + 1) * PART], rounded, (((1,), (1,)), ((), ())),
+            preferred_element_type=jnp.float32,
+        )
+
+
+def per_device(images, expansion_basis, block_sizes, keep_count, start_block):
     plan = Plan()
     rows = images.shape[0]
-    own = jnp.pad(basis.T, ((0, ROWS - basis.shape[1]), (0, 0)))
+    scale = 1.0 / (2 * rows * 128)
+    own = jnp.pad(expansion_basis.T, ((0, ROWS - expansion_basis.shape[1]), (0, 0)))
     own = own.reshape(ROWS, CHUNKS, KC).swapaxes(0, 1)
     any_ = pl.BlockSpec(memory_space=pl.ANY)
-    return pl.pallas_call(
+    scalars = pl.BlockSpec(memory_space=pltpu.SMEM)
+    vmem = pl.BlockSpec(memory_space=pltpu.VMEM)
+    tiles = (3, 32, 128)
+    f32 = jnp.float32
+    coeffs = pl.pallas_call(
         functools.partial(gather_dot, plan),
-        out_shape=jax.ShapeDtypeStruct((rows, 32 * ROWS), jnp.bfloat16),
+        out_shape=jax.ShapeDtypeStruct((rows, 2 * PART), jnp.bfloat16),
         in_specs=[any_, any_],
-        out_specs=pl.BlockSpec(memory_space=pltpu.VMEM),
+        out_specs=vmem,
         scratch_shapes=[
             pltpu.VMEM((CHUNKS, 4, 4, 2, ROWS, KC), jnp.bfloat16),
             pltpu.VMEM(images.shape, jnp.bfloat16),
-            pltpu.VMEM((rows, 32 * ROWS), jnp.float32),
+            pltpu.VMEM((rows, 2 * PART), f32),
             pltpu.SemaphoreType.DMA((3,)),
             pltpu.SemaphoreType.DMA,
             pltpu.SemaphoreType.DMA((len(plan.sems),)),
         ],
         compiler_params=pltpu.CompilerParams(
-            collective_id=0, has_side_effects=True, vmem_limit_bytes=48 * 1024 * 1024
+            collective_id=0, has_side_effects=True, vmem_limit_bytes=58 * 1024 * 1024
         ),
     )(images, own)
-
-
-def cut_along(shard, dim, peers):
-    shape = shard.shape
-    tiles = shard.reshape(*shape[:dim], peers, shape[dim] // peers, *shape[dim + 1 :])
-    return jnp.moveaxis(tiles, dim, 0)
-
-
-def sum_at_owner(shard, axis, dim):
-    peers = lax.axis_size(axis)
-    tiles = lax.all_to_all(cut_along(shard, dim, peers), axis, 0, 0, tiled=True)
-    return jnp.sum(tiles, axis=0)
-
-
-def summed_rows(shard, axes, dim):
-    far, near = axes
-    tiles = cut_along(shard, dim, lax.axis_size(far))
-    nearer = sum_at_owner(tiles, near, dim + 1)
-    arrived = lax.all_to_all(nearer, far, split_axis=0, concat_axis=0, tiled=True)
-    return arrived.sum(axis=0)
-
-
-def padded_to(lines, peers):
-    spare = -len(lines) % peers
-    return jnp.pad(lines, [(0, spare)] + [(0, 0)] * (lines.ndim - 1))
-
-
-def sent_to_all(shard, axis):
-    peers = lax.axis_size(axis)
-    return lax.all_to_all(
-        jnp.broadcast_to(shard[None], (peers, *shard.shape)), axis, 0, 0, tiled=True
-    )
-
-
-def in_order(tiles, dim):
-    shape = list(tiles.shape[1:])
-    shape[dim] *= tiles.shape[0]
-    return jnp.moveaxis(tiles, 0, dim).reshape(shape)
-
-
-def gather_axes(shard, axes, dim):
-    far, near = axes
-    leading = sent_to_all(shard, far)
-    tiles = jnp.swapaxes(sent_to_all(leading, near), 0, 1)
-    return in_order(tiles.reshape(-1, *shard.shape), dim)
-
-
-def nested_sum(shard, axes):
-    lines = shard.reshape(-1, shard.shape[-1])
-    own = summed_rows(padded_to(lines, lax.axis_size(axes[0]) * lax.axis_size(axes[1])), axes, 0)
-    whole = gather_axes(own, axes, 0)
-    return whole[: len(lines)].reshape(shard.shape)
-
-
-def selector(block_sizes, count, width):
-    offsets = jnp.cumsum(block_sizes) - block_sizes
-    place = jnp.arange(16 * ROWS, dtype=jnp.int32)
-    column = jnp.where(place % ROWS < 30, place // ROWS * 30 + place % ROWS, -1)[:, None, None]
-    inside = jnp.arange(width, dtype=jnp.int32)[None, None, :]
-    hit = (column == offsets[None, :, None] + inside) & (inside < block_sizes[None, :, None])
-    return hit.astype(jnp.bfloat16).reshape(16 * ROWS, count * width)
-
-
-def subspace(cover, block_sizes, keep_count, start_block):
-    width = cover.shape[1]
-    ranks = start_block.shape[2]
-    inside = jnp.arange(width, dtype=jnp.int32)[None, :, None] < block_sizes[:, None, None]
-    keep = jnp.minimum(keep_count, (block_sizes + 1) // 2)
-    current = jnp.where(inside, start_block, jnp.zeros_like(start_block))
-    for turn in range(ITERS):
-        product = jnp.einsum("bij,bjk->bik", cover, current, precision=HIGH)
-        columns = []
-        for column_id in range(ranks):
-            vector = product[:, :, column_id]
-            for earlier in columns:
-                vector = vector - jnp.sum(earlier * vector, axis=1, keepdims=True) * earlier
-            length = jnp.sqrt(jnp.sum(vector * vector, axis=1, keepdims=True))
-            alive = (column_id < keep)[:, None]
-            columns.append(jnp.where(alive, vector / length, jnp.zeros_like(vector)))
-        current = jnp.stack(columns, axis=2)
-    product = jnp.einsum("bij,bjk->bik", cover, current, precision=HIGH)
-    found = jnp.sum(current * product, axis=1)
-    return (current, found)
-
-
-def per_device(images, expansion_basis, block_sizes, keep_count, start_block):
-    rows = images.shape[0]
-    coeffs = gathered_coeffs(images, expansion_basis)
-    samples = coeffs.reshape(2 * rows, 16 * ROWS)
-    pick = selector(block_sizes, L, NMAX)
-    padded = jnp.dot(samples, pick, preferred_element_type=jnp.float32).astype(jnp.bfloat16)
-    wide = padded.reshape(2 * rows, L, NMAX)
-    scale = 1.0 / (2 * rows * lax.axis_size(IMG) * lax.axis_size("grp"))
-    partial_value = (
-        jnp.einsum("rli,rlj->lij", wide, wide, preferred_element_type=jnp.float32) * scale
-    )
-    cover = nested_sum(partial_value, (("img_0", "img_1"), ("img_2", "grp")))
-    vectors, found = subspace(cover, block_sizes, keep_count, start_block)
-    rounded = vectors.astype(jnp.bfloat16)
-    features = jnp.einsum("rli,lij->rlj", wide, rounded, preferred_element_type=jnp.float32)
-    return (features.reshape(rows, 2 * L * KMAX), found)
+    packed, begin = pl.pallas_call(
+        cut_windows,
+        out_shape=(jax.ShapeDtypeStruct((4, 2, *tiles), f32), jax.ShapeDtypeStruct((3, L * KMAX, 128), f32)),
+        in_specs=[scalars, scalars, vmem, vmem],
+        out_specs=(vmem, vmem),
+        scratch_shapes=[pltpu.VMEM((PART, PART), f32)],
+        compiler_params=pltpu.CompilerParams(vmem_limit_bytes=16 * 1024 * 1024),
+    )(block_sizes, keep_count, coeffs, start_block.swapaxes(1, 2))
+    everything = pl.pallas_call(
+        functools.partial(reduce_iterate, scale),
+        out_shape=jax.ShapeDtypeStruct((L * KMAX, 128), f32),
+        in_specs=[vmem, vmem],
+        out_specs=vmem,
+        scratch_shapes=[
+            pltpu.VMEM((4, *tiles), f32),
+            pltpu.VMEM((4, *tiles), f32),
+            pltpu.VMEM((3, *tiles), f32),
+            pltpu.VMEM((4, *tiles), f32),
+            pltpu.VMEM((4, *tiles), f32),
+            pltpu.VMEM((8, 2 * KMAX, 128), f32),
+            pltpu.SemaphoreType.DMA((2,)),
+            pltpu.SemaphoreType.DMA((6, 3)),
+            pltpu.SemaphoreType.DMA((2, 7)),
+        ],
+        compiler_params=pltpu.CompilerParams(
+            collective_id=1, has_side_effects=True, vmem_limit_bytes=16 * 1024 * 1024
+        ),
+    )(packed, begin)
+    return pl.pallas_call(
+        project,
+        out_shape=(
+            jax.ShapeDtypeStruct((rows, 2 * L * KMAX), f32),
+            jax.ShapeDtypeStruct((L, KMAX), f32),
+        ),
+        in_specs=[scalars, vmem, vmem],
+        out_specs=(vmem, vmem),
+        compiler_params=pltpu.CompilerParams(vmem_limit_bytes=16 * 1024 * 1024),
+    )(block_sizes, coeffs, everything)
 
 
 def solution(mesh):
-    split = Mesh(
-        mesh.devices.reshape(4, 4, 2, mesh.shape["grp"]), ("img_0", "img_1", "img_2", "grp")
-    )
-    in_specs = (P(IMG_GRP, None), P(None, IMG), P(), P(), P())
-    out_specs = (P(IMG_GRP, None), P())
+    split = Mesh(mesh.devices.reshape(4, 4, 2, mesh.shape["grp"]), AXES)
+    in_specs = (P(AXES, None), P(None, IMG), P(), P(), P())
+    out_specs = (P(AXES, None), P())
     return jax.shard_map(
         per_device, mesh=split, in_specs=in_specs, out_specs=out_specs, check_vma=False
     )

time: 153 us -> 89.1 us (0.58)
  Pallas kernels: 54.2 us -> 83.2 us
  blocking collectives: 25 us -> 0 us
  waiting for transfers between devices: 17.1 us -> 0 us
  other arithmetic: 15.9 us -> 0 us
  local copies, waits for them, and re-layouts: 20.2 us -> 4.96 us
  starting transfers between devices: 9.94 us -> 0 us
  matrix products: 8.76 us -> 0 us
    pallas_call x1 -> x4, Pallas kernels: 54.2 us -> 83.2 us  [the longest x1 54.9 us: per_device(): pl.pallas_call(functools.partial(gather_dot, plan), out_shape=jax.ShapeDt...]
    all_to_all x2 -> x0, blocking collectives: 25 us -> none  [the longest x1 13.6 us: sum_at_owner(): tiles = lax.all_to_all(cut_along(shard, dim, peers), axis, 0, 0, tiled=True)]
    all_to_all x2 -> x0, waiting for transfers between devices: 17.1 us -> none  [sent_to_all(): lax.all_to_all(jnp.broadcast_to(shard[None], (peers, *shard.shape)), axis...]
    reduce_sum x48 -> x0, other arithmetic: 10.2 us -> none  [the longest x30 6.8 us: subspace(): vector = vector - jnp.sum(earlier * vector, axis=1, keepdims=True) * earlier]
    all_to_all x2 -> x0, starting transfers between devices: 9.94 us -> none  [sent_to_all(): lax.all_to_all(jnp.broadcast_to(shard[None], (peers, *shard.shape)), axis...]
    dot_general x7 -> x0, matrix products: 8.76 us -> none  [the longest x4 5.13 us: subspace(): product = jnp.einsum('bij,bjk->bik', cover, current, precision=HIGH)]
    reshape x3 -> x1, local copies, waits for them, and re-layouts: 6.63 us -> 0.9 us  [per_device(): own = own.reshape(ROWS, CHUNKS, KC).swapaxes(0, 1)]
    transpose x1 -> x0, local copies, waits for them, and re-layouts: 4.86 us -> none  [per_device(): jnp.einsum('rli,lij->rlj', wide, rounded, preferred_element_type=jnp.floa...]
  transfers between devices with their start and end apart: 2 -> 0, of which waited for: 2 -> 0; matrix products, arithmetic and copies ran while one was open for 0% -> 0% of each run, Pallas kernels for 0% -> 0%
where the time goes in v2:
time: 89.1 us; the launch traced here: 88.9 us
  Pallas kernels  83.2 us (93%)
  local copies, waits for them, and re-layouts  4.96 us (6%)
    pallas_call x1, Pallas kernels, per_device(): pl.pallas_call(functools.partial(gather_dot, plan), out_shape=jax.ShapeDt...  54.9 us
    pallas_call x1, Pallas kernels, per_device(): pl.pallas_call(functools.partial(reduce_iterate, scale), out_shape=jax.Sh...  24.5 us
    unnamed x10, local copies, waits for them, and re-layouts  2.27 us
    pallas_call x1, Pallas kernels, per_device(): pl.pallas_call(cut_windows, out_shape=(jax.ShapeDtypeStruct((4, 2, *tiles...  1.92 us
    pallas_call x1, Pallas kernels, per_device(): pl.pallas_call(project, out_shape=(jax.ShapeDtypeStruct((rows, 2 * L * KM...  1.86 us

profile of v2, /device:TPU:1, one launch (start us, length us, event | category | flops | bytes accessed | tf_op | source)
XLA Modules:
  0.0 88.9 jit_solution(6692158623493523440)
XLA Ops:
  0.6 0.0 copy-start.3
  0.6 0.0 copy-start.2
  0.7 0.0 copy-start.4
  0.7 1.1 %pad.4 = bf16[32,9216]{1,0:T(8,128)(2,1)S(1)} pad(bf16[30,9216]{1,0:T(8,128)(2,1)} %bitcast.12, bf16[]{:T(256)} %constant.2.clone.1), padding=0_2x0_0 | pad | bytes 1142786 | tf_op jit(solution)/shard_map/jit(_pad)/pad | solution.py:384
  1.8 0.9 %copy.12 = bf16[4,36,8,256]{3,2,0,1:T(8,128)(2,1)} copy(bf16[4,36,8,256]{3,2,1,0:T(8,128)(2,1)S(1)} %bitcast.11) | data formatting | bytes 1179648 | tf_op jit(solution)/shard_map/reshape | solution.py:385
  2.7 54.9 %shard_map.68.coeffs = bf16[384,1024]{1,0:T(8,128)(2,1)} custom-call(bf16[384,9216]{1,0:T(8,128)(2,1)} %images.1, bf16[36,32,256]{2,1,0:T(8,128)(2,1)} %bitcast.10), custom_call_target="tpu_custom_call" | custom-call | tf_op jit(solution)/shard_map/pallas_call | solution.py:391
  57.6 0.0 copy-done.3
  57.6 0.0 copy-done.2
  57.7 0.0 copy-done.4
  57.7 0.0 copy-start
  57.7 1.1 %copy-done = bf16[384,1024]{1,0:T(8,128)(2,1)S(1)} copy-done((bf16[384,1024]{1,0:T(8,128)(2,1)S(1)}, bf16[384,1024]{1,0:T(8,128)(2,1)}, u32[]{:S(2)}) %copy-start) | copy-done | bytes 786456
  58.8 1.9 %shard_map.69 = (f32[4,2,3,32,128]{4,3,2,1,0:T(8,128)S(1)}, f32[3,128,128]{2,1,0:T(8,128)S(1)}) custom-call(s32[16]{0:T(128)S(1)} %copy-done.3, s32[16]{0:T(128)S(1)} %copy-done.4, bf16[384,1024]{1,0:T(8,128)(2,1)S(1)} %copy-done, f32[16,8,80]{2,1,0:T(8,128)S(1)} %bitcast.9), custom_call_target="tpu_custom_call" | custom-call | tf_op jit(solution)/shard_map/pallas_call | solution.py:408
  60.7 24.5 %shard_map.70.everything = f32[128,128]{1,0:T(8,128)S(1)} custom-call(f32[4,2,3,32,128]{4,3,2,1,0:T(8,128)S(1)} %get-tuple-element.4.packed, f32[3,128,128]{2,1,0:T(8,128)S(1)} %get-tuple-element.5.begin), custom_call_target="tpu_custom_call" | custom-call | tf_op jit(solution)/shard_map/pallas_call | solution.py:416
  85.2 0.0 copy-start.1
  85.3 1.1 %copy-done.1 = bf16[384,1024]{1,0:T(8,128)(2,1)S(1)} copy-done((bf16[384,1024]{1,0:T(8,128)(2,1)S(1)}, bf16[384,1024]{1,0:T(8,128)(2,1)}, u32[]{:S(2)}) %copy-start.1) | copy-done | bytes 786456
  86.4 1.9 %shard_map.71 = (f32[384,256]{1,0:T(8,128)}, f32[16,8]{1,0:T(8,128)S(1)}) custom-call(s32[16]{0:T(128)S(1)} %copy-done.3, bf16[384,1024]{1,0:T(8,128)(2,1)S(1)} %copy-done.1, f32[128,128]{1,0:T(8,128)S(1)} %shard_map.70.everything), custom_call_target="tpu_custom_call" | custom-call | tf_op jit(solution)/shard_map/pallas_call | solution.py:436
  88.2 0.7 copy.9
Async XLA Ops:
  0.6 57.0 %copy-start.3 = (s32[16]{0:T(128)S(1)}, s32[16]{0:T(128)}, u32[]{:S(2)}) copy-start(s32[16]{0:T(128)} %sizes.3) | copy-start | bytes 196
  0.6 57.0 %copy-start.2 = (f32[16,80,8]{1,2,0:T(8,128)S(1)}, f32[16,80,8]{1,2,0:T(8,128)}, u32[]{:S(2)}) copy-start(f32[16,80,8]{1,2,0:T(8,128)} %param.9) | copy-start | bytes 122884
  0.7 57.0 %copy-start.4 = (s32[16]{0:T(128)S(1)}, s32[16]{0:T(128)}, u32[]{:S(2)}) copy-start(s32[16]{0:T(128)} %keeps.1) | copy-start | bytes 196
  57.7 1.1 %copy-start = (bf16[384,1024]{1,0:T(8,128)(2,1)S(1)}, bf16[384,1024]{1,0:T(8,128)(2,1)}, u32[]{:S(2)}) copy-start(bf16[384,1024]{1,0:T(8,128)(2,1)} %shard_map.68.coeffs) | copy-start | bytes 2359300
  85.2 1.1 %copy-start.1 = (bf16[384,1024]{1,0:T(8,128)(2,1)S(1)}, bf16[384,1024]{1,0:T(8,128)(2,1)}, u32[]{:S(2)}) copy-start(bf16[384,1024]{1,0:T(8,128)(2,1)} %shard_map.68.coeffs) | copy-start | bytes 2359300

commit v3 on v2

v3 whole, which is shorter than its diff:
```python
import functools
import heapq

import jax
import jax.numpy as jnp
from jax import lax
from jax.experimental import pallas as pl
from jax.experimental.pallas import tpu as pltpu
from jax.sharding import Mesh
from jax.sharding import PartitionSpec as P

NMAX = 80
L = 16
S = 480
KMAX = 8
ITERS = 3
AXES = ("img_0", "img_1", "img_2", "grp")
IMG = AXES[:3]
HIGH = lax.Precision.HIGHEST
MESH = pl.DeviceIdType.MESH

KC = 256
SUBS = 4
SIZES = (1, 2, 1, 1, 1)
CHUNKS = 36
ROWS = 32
BLOCK = ROWS * KC * 2
PART = 16 * ROWS
WIN = 96


class Plan:
    def __init__(
        self, window=2.5, late=0.3, turns=0.5, rate=42.5e3, hop=2.8, d_rate=600e3, d_hop=1.4, dot=0.25, queue=3
    ):
        self.program = []
        self.sems = {}
        self.now = 0.0
        busy, pending, arrived = {}, {}, {}
        heap, ready = [], []
        count = iter(range(10**6))

        def to_go(key):
            r, sub, da, db, dx = key
            forward = -1 if sub % 2 == 0 else 1
            if dx:
                return 1 if dx == forward else 0
            hops = 2 if r == 0 else 0
            if db == 0:
                return hops + 2 + (da == forward)
            return hops + (db == forward)

        def issue(key, link, size):
            sem = self.sems.setdefault(key, len(self.sems))
            end = max(busy.get(link, 0.0), self.now) + size / (d_rate if link == "d" else rate)
            busy[link] = end
            heapq.heappush(heap, (end + (d_hop if link == "d" else hop), sem, key))
            self.program.append(("send", key))

        def pump():
            for link, line in pending.items():
                while line and busy.get(link, 0.0) < self.now + window:
                    _, _, key, size = heapq.heappop(line)
                    issue(key, link, size)

        def along(axis, place, at, key):
            forward = -1 if key[1] % 2 == 0 else 1
            if place == 0:
                steps = ((-1, "+"), (1, "-"))
            elif place == forward:
                steps = ((2, "+" if forward == -1 else "-"),)
            else:
                steps = ()
            for there, sign in steps:
                onto = key[:at] + (there,) + key[at + 1 :]
                rank = onto[0] * late + onto[1] * turns - to_go(onto)
                line = pending.setdefault(axis + sign, [])
                heapq.heappush(line, (rank, next(count), onto, SIZES[key[0]] * BLOCK))

        def onward(key):
            r, sub, da, db, dx = key
            first, second = ("y", "z") if sub < 2 else ("z", "y")
            if dx == 0:
                if db == 0:
                    along(first, da, 2, key)
                along(second, db, 3, key)
            if r == 0 and (da, db) != (0, 0):
                along("x", dx, 4, key)

        def got(group, need):
            arrived[group] = arrived.get(group, 0) + 1
            return arrived[group] == need

        for r in range(len(SIZES)):
            for sub in range(SUBS):
                onward((r, sub, 0, 0, 0))
        pump()
        while heap or ready:
            if ready and (not heap or heap[0][0] > self.now or len(ready) > queue):
                self.program.append(("dot", ready.pop(0)))
                self.now += dot
            else:
                when, _, key = heapq.heappop(heap)
                self.now = max(self.now, when) + 0.02
                self.program.append(("wait", key))
                if key[0] == "D":
                    chunk = key[1:4]
                else:
                    onward(key)
                    chunk = (key[0], key[1], key[4])
                    if got((*chunk, "line", key[3]), 4 if key[3] else 3):
                        issue(("D", *chunk, key[3]), "d", 4 * BLOCK * SIZES[key[0]])
                if got(chunk, 19):
                    ready.extend((*chunk, k) for k in range(SIZES[chunk[0]]))
            pump()
        self.end = self.now


def turn(v, by):
    return lax.rem(v + (by + 4), 4)


def device(axis, by):
    spot = dict(zip("yzcx", (lax.axis_index(a) for a in AXES)))
    spot[axis] = turn(spot[axis], by)
    return tuple(spot[a] for a in "yzcx")


def gather_dot(plan, images, basis, coeffs, held, pixels, total, fill_sem, send_sem, recv_sem):
    y, z, c, x = (lax.axis_index(a) for a in AXES)
    sibling = (y, z, 1 - c, x)
    barrier = pltpu.get_barrier_semaphore()
    for peer in [device(axis, by) for axis in "yzx" for by in (1, -1)] + [sibling]:
        pl.semaphore_signal(barrier, inc=1, device_id=peer, device_id_type=MESH)
    fill = pltpu.make_async_copy(images, pixels, fill_sem)
    fill.start()
    for k in range(CHUNKS):
        held[k, y, z, c] = jnp.zeros((ROWS, KC), jnp.bfloat16)
        held[k, y, z, c, : basis.shape[0]] = basis[:, k * KC : (k + 1) * KC]
    total[...] = jnp.zeros_like(total)
    pl.semaphore_wait(barrier, 7)

    def index(r, sub, dx):
        if r == 0:
            return SUBS * turn(x, dx) + sub
        return SUBS * (4 + sum(SIZES[1:r])) + sub * SIZES[r]

    def copy_of(key):
        if key[0] == "D":
            r, sub, dx, db = key[1:]
            k = pl.ds(index(r, sub, dx), SIZES[r])
            part = held.at[k, :, turn(z, db), c] if sub < 2 else held.at[k, turn(y, db), :, c]
            where = sibling
        else:
            r, sub = key[:2]
            place = list(key[2:])
            moving = 2 if place[2] else 1 if place[1] else 0
            forward = -1 if sub % 2 == 0 else 1
            there = place[moving]
            step = -there if there != 2 else -forward
            place[moving] = 0 if there != 2 else forward
            da, db, dx = place
            dy, dz = (da, db) if sub < 2 else (db, da)
            part = held.at[pl.ds(index(r, sub, dx), SIZES[r]), turn(y, dy), turn(z, dz), c]
            where = device(("yzx" if sub < 2 else "zyx")[moving], step)
        return pltpu.make_async_remote_copy(
            src_ref=part, dst_ref=part, send_sem=send_sem, recv_sem=recv_sem.at[plan.sems[key]],
            device_id=where, device_id_type=MESH,
        )

    sent = []
    loaded = False
    for op, what in plan.program:
        if op == "send":
            copy = copy_of(what)
            copy.start()
            sent.append(copy)
        elif op == "wait":
            copy_of(what).wait_recv()
        else:
            if not loaded:
                fill.wait()
                loaded = True
            k = index(*what[:3]) + what[3]
            block = held[k].reshape(32 * ROWS, KC)
            rows = pixels[:, pl.ds(pl.multiple_of(k * KC, KC), KC)]
            total[...] += lax.dot_general(
                rows, block, (((1,), (1,)), ((), ())), preferred_element_type=jnp.float32
            )
    if not loaded:
        fill.wait()
    for copy in sent:
        copy.wait_send()
    coeffs[...] = total[...].astype(coeffs.dtype)


def places(sizes):
    offsets, firsts = [], []
    offset = jnp.int32(0)
    for l in range(L):
        offsets.append(offset)
        place = lax.div(offset, 30) * ROWS + lax.rem(offset, 30)
        firsts.append(jnp.minimum(lax.div(place, 8) * 8, PART - WIN))
        offset = offset + sizes[l]
    return offsets, firsts


def cut_windows(sizes, keeps, coeffs, start, packed, begin, gram):
    def part_gram(p):
        some = coeffs[:, p * PART : (p + 1) * PART]
        return lax.dot_general(some, some, (((0,), (0,)), ((), ())), preferred_element_type=jnp.float32)

    gram[...] = part_gram(0) + part_gram(1)

    offsets, firsts = places(sizes)

    def window(l):
        left = jnp.minimum(lax.div(firsts[l], 128), 2) * 128
        rows = gram[pl.ds(pl.multiple_of(firsts[l], 8), WIN), pl.ds(pl.multiple_of(left, 128), 256)]
        return pltpu.roll(rows, lax.rem(256 - (firsts[l] - left), 256), 1)[:, :128]

    lane = lax.broadcasted_iota(jnp.int32, (32, 128), 1)
    for pair in range(L // 2):
        one, two = window(2 * pair), window(2 * pair + 1)
        xo, co = pair // 2, pair % 2
        packed[xo, co, 0] = jnp.where(lane < 96, one[:32], pltpu.roll(one[64:], 32, 1))
        packed[xo, co, 1] = jnp.where(lane < 96, two[:32], pltpu.roll(two[64:], 32, 1))
        packed[xo, co, 2] = jnp.where(lane < 64, pltpu.roll(one[32:64], 96, 1), pltpu.roll(two[32:64], 32, 1))

    row = lax.broadcasted_iota(jnp.int32, (KMAX, 128), 0)
    place = lax.broadcasted_iota(jnp.int32, (NMAX, 128), 1)
    inner = lax.broadcasted_iota(jnp.int32, (NMAX, 128), 0)
    for l in range(L):
        slot = lax.rem(firsts[l] + place, ROWS)
        source = lax.div(firsts[l] + place, ROWS) * 30 + slot - offsets[l]
        source = jnp.where(slot < 30, source, -1)
        hit = ((source == inner) & (inner < sizes[l])).astype(jnp.float32)
        lines = slice(KMAX * l, KMAX * l + KMAX)
        begin[0, lines] = jnp.dot(start[l], hit, precision=HIGH, preferred_element_type=jnp.float32)
        begin[1, lines] = jnp.broadcast_to(jnp.sum(hit, axis=0, keepdims=True), (KMAX, 128))
        keep = jnp.minimum(keeps[l], lax.div(sizes[l] + 1, 2))
        begin[2, lines] = (row < keep).astype(jnp.float32)


def iterate(summed, current, inside, alive):
    wide = lax.broadcasted_iota(jnp.int32, (128, 128), 1)
    block_row = lax.div(lax.broadcasted_iota(jnp.int32, (128, 128), 0), 32) * 32

    def cover_of(i):
        low = jnp.zeros((32, 128), jnp.float32)
        middle = pltpu.roll(summed[2], 32 if i == 0 else 96, 1)
        upper = jnp.concatenate([summed[i], middle, pltpu.roll(summed[i], 96, 1), low], axis=0)
        upper = jnp.where((wide >= block_row) & (wide < WIN), upper, 0.0)
        beyond = jnp.where(wide >= block_row + 32, upper, 0.0)
        return upper + beyond.T

    row = lax.broadcasted_iota(jnp.int32, (KMAX, 128), 0)
    column = lax.broadcasted_iota(jnp.int32, (KMAX, 128), 1)

    def times(current, cover):
        return jnp.dot(current, cover, precision=HIGH, preferred_element_type=jnp.float32)

    covers = [cover_of(i) for i in range(2)]
    lines = [slice(KMAX * i, KMAX * i + KMAX) for i in range(2)]
    currents = [current[i] for i in lines]
    inside = [inside[i] > 0.5 for i in lines]
    alive = [alive[i] > 0.5 for i in lines]
    for turn_id in range(ITERS):
        stacks = [jnp.where(inside[i], times(currents[i], covers[i]), 0.0) for i in range(2)]
        norms = [jnp.ones((KMAX, 1), jnp.float32) for _ in range(2)]
        for m in range(KMAX):
            for i in range(2):
                vector = stacks[i][m : m + 1]
                dots = jnp.sum(stacks[i] * vector, axis=1, keepdims=True)
                square = dots[m : m + 1]
                norms[i] = jnp.where(row[:, :1] == m, square, norms[i])
                if m < KMAX - 1:
                    stacks[i] = jnp.where(row > m, stacks[i] - dots / square * vector, stacks[i])
        currents = [jnp.where(alive[i], stacks[i] / jnp.sqrt(norms[i]), 0.0) for i in range(2)]
    ends = []
    for i in range(2):
        quotient = jnp.sum(currents[i] * times(currents[i], covers[i]), axis=1, keepdims=True)
        ends.append(jnp.where(column == 127, quotient, currents[i]))
    return jnp.concatenate(ends, axis=0)


def reduce_iterate(scale, packed, begin, everything, mate, half, by_x, one, two, found, mate_sem, far_sem, found_sem):
    y, z, c, x = (lax.axis_index(a) for a in AXES)
    sibling = (y, z, 1 - c, x)
    owners = [device("x", by) for by in (1, 2, 3)] + [(y, z, 1 - c, turn(x, by)) for by in range(4)]
    barrier = pltpu.get_barrier_semaphore()
    for peer in owners + [device(axis, by) for axis in "yz" for by in (1, 2, 3)]:
        pl.semaphore_signal(barrier, inc=1, device_id=peer, device_id_type=MESH)
    pl.semaphore_wait(barrier, 13)
    sent = []

    def push(src, dst, sems, where):
        copy = pltpu.make_async_remote_copy(
            src_ref=src, dst_ref=dst, send_sem=sems[0], recv_sem=sems[1], device_id=where, device_id_type=MESH
        )
        copy.start()
        sent.append(copy)
        return copy

    def far(stage, h):
        return [(far_sem.at[stage, h, 0, by - 1], far_sem.at[stage, h, 1, by - 1]) for by in (1, 2, 3)]

    push(packed.at[:, 1 - c], mate, (mate_sem.at[0], mate_sem.at[1]), sibling).wait_recv()
    copies = []
    for h in range(2):
        lines = slice(16 * h, 16 * h + 16)
        for xo in range(4):
            half[h, xo] = packed[xo, c, :, lines] + mate[xo, :, lines]
        copies.append([
            push(half.at[h, turn(x, by)], by_x.at[h, by - 1], far(0, h)[by - 1], device("x", by)) for by in (1, 2, 3)
        ])
    for stage, (land, spots, axes) in enumerate(((one, (y, z), "yz"), (two, (z, y), "zy"))):
        onward = []
        for h in range(2):
            for copy in copies[h]:
                copy.wait_recv()
            spot = spots[h]
            if stage == 0:
                land[h, spot] = half[h, x] + by_x[h, 0] + by_x[h, 1] + by_x[h, 2]
            else:
                land[h, spot] = one[h, 0] + one[h, 1] + one[h, 2] + one[h, 3]
            onward.append([
                push(land.at[h, spot], land.at[h, spot], far(1 + stage, h)[by - 1], device(axes[h], by))
                for by in (1, 2, 3)
            ])
        copies = onward
    for h in range(2):
        for copy in copies[h]:
            copy.wait_recv()
    sums = [two[h, 0] + two[h, 1] + two[h, 2] + two[h, 3] for h in range(2)]
    summed = jnp.concatenate(sums, axis=1) * scale

    me = 2 * x + c
    lines = pl.ds(pl.multiple_of(2 * KMAX * me, 2 * KMAX), 2 * KMAX)
    found[me] = iterate(summed, begin[0, lines], begin[1, lines], begin[2, lines])
    copies = [push(found.at[me], found.at[me], (found_sem.at[0, e], found_sem.at[1, e]), owners[e]) for e in range(7)]
    for copy in copies:
        copy.wait_recv()
    everything[...] = found[...].reshape(L * KMAX, 128)
    for copy in sent:
        copy.wait_send()


def project(sizes, coeffs, everything, features, values):
    firsts = places(sizes)[1]
    tall = lax.broadcasted_iota(jnp.int32, (L * KMAX, 128), 0)
    wide = lax.broadcasted_iota(jnp.int32, (L * KMAX, 128), 1)
    spread = jnp.where(lax.div(tall, KMAX) == wide, everything[:, 127:128], 0.0)
    choose = lax.rem(wide[:KMAX], KMAX) == tall[:KMAX]
    values[...] = jnp.dot(
        choose.astype(jnp.float32), spread, precision=HIGH, preferred_element_type=jnp.float32
    )[:, :L]
    lines = []
    for l in range(L):
        line = jnp.where(wide[:KMAX] < WIN, everything[KMAX * l : KMAX * l + KMAX], 0.0)
        line = jnp.concatenate([line, jnp.zeros((KMAX, PART - 128), jnp.float32)], axis=1)
        lines.append(pltpu.roll(line, firsts[l], 1))
    rounded = jnp.concatenate(lines, axis=0).astype(jnp.bfloat16)
    for p in range(2):
        features[:, p * 128 : (p + 1) * 128] = lax.dot_general(
            coeffs[:, p * PART : (p + 1) * PART], rounded, (((1,), (1,)), ((), ())),
            preferred_element_type=jnp.float32,
        )


def per_device(images, expansion_basis, block_sizes, keep_count, start_block):
    plan = Plan()
    rows = images.shape[0]
    scale = 1.0 / (2 * rows * 128)
    scalars = pl.BlockSpec(memory_space=pltpu.SMEM)
    vmem = pl.BlockSpec(memory_space=pltpu.VMEM)
    f32, bf16 = jnp.float32, jnp.bfloat16
    tiles, halves = (3, 32, 128), (3, 16, 128)
    coeffs = pl.pallas_call(
        functools.partial(gather_dot, plan),
        out_shape=jax.ShapeDtypeStruct((rows, 2 * PART), bf16),
        in_specs=[pl.BlockSpec(memory_space=pltpu.HBM), vmem],
        out_specs=vmem,
        scratch_shapes=[
            pltpu.VMEM((CHUNKS, 4, 4, 2, ROWS, KC), bf16),
            pltpu.VMEM(images.shape, bf16),
            pltpu.VMEM((rows, 2 * PART), f32),
            pltpu.SemaphoreType.DMA,
            pltpu.SemaphoreType.DMA,
            pltpu.SemaphoreType.DMA((len(plan.sems),)),
        ],
        compiler_params=pltpu.CompilerParams(
            collective_id=0, has_side_effects=True, vmem_limit_bytes=52 * 1024 * 1024
        ),
    )(images, expansion_basis.T)
    packed, begin = pl.pallas_call(
        cut_windows,
        out_shape=(jax.ShapeDtypeStruct((4, 2, *tiles), f32), jax.ShapeDtypeStruct((3, L * KMAX, 128), f32)),
        in_specs=[scalars, scalars, vmem, vmem],
        out_specs=(vmem, vmem),
        scratch_shapes=[pltpu.VMEM((PART, PART), f32)],
        compiler_params=pltpu.CompilerParams(vmem_limit_bytes=16 * 1024 * 1024),
    )(block_sizes, keep_count, coeffs, start_block.swapaxes(1, 2))
    everything = pl.pallas_call(
        functools.partial(reduce_iterate, scale),
        out_shape=jax.ShapeDtypeStruct((L * KMAX, 128), f32),
        in_specs=[vmem, vmem],
        out_specs=vmem,
        scratch_shapes=[
            pltpu.VMEM((4, *tiles), f32),
            pltpu.VMEM((2, 4, *halves), f32),
            pltpu.VMEM((2, 3, *halves), f32),
            pltpu.VMEM((2, 4, *halves), f32),
            pltpu.VMEM((2, 4, *halves), f32),
            pltpu.VMEM((8, 2 * KMAX, 128), f32),
            pltpu.SemaphoreType.DMA((2,)),
            pltpu.SemaphoreType.DMA((3, 2, 2, 3)),
            pltpu.SemaphoreType.DMA((2, 7)),
        ],
        compiler_params=pltpu.CompilerParams(
            collective_id=1, has_side_effects=True, vmem_limit_bytes=16 * 1024 * 1024
        ),
    )(packed, begin)
    features, values = pl.pallas_call(
        project,
        out_shape=(
            jax.ShapeDtypeStruct((rows, 2 * L * KMAX), f32),
            jax.ShapeDtypeStruct((KMAX, L), f32),
        ),
        in_specs=[scalars, vmem, vmem],
        out_specs=(vmem, vmem),
        compiler_params=pltpu.CompilerParams(vmem_limit_bytes=16 * 1024 * 1024),
    )(block_sizes, coeffs, everything)
    return features, values.T


def solution(mesh):
    split = Mesh(mesh.devices.reshape(4, 4, 2, mesh.shape["grp"]), AXES)
    in_specs = (P(AXES, None), P(None, IMG), P(), P(), P())
    out_specs = (P(AXES, None), P())
    return jax.shard_map(
        per_device, mesh=split, in_specs=in_specs, out_specs=out_specs, check_vma=False
    )
```

time: 89.1 us -> 79.8 us (0.90)
  Pallas kernels: 83.2 us -> 77.9 us
  local copies, waits for them, and re-layouts: 4.96 us -> 1.08 us
    pallas_call x1, Pallas kernels: 54.9 us -> 51.4 us  [per_device(): pl.pallas_call(functools.partial(gather_dot, plan), out_shape=jax.ShapeDt...]
    pallas_call x1, Pallas kernels: 24.5 us -> 22.7 us  [per_device(): pl.pallas_call(functools.partial(reduce_iterate, scale), out_shape=jax.Sh...]
    unnamed x10 -> x8, local copies, waits for them, and re-layouts: 2.27 us -> 1.08 us
    pad x1 -> x0, local copies, waits for them, and re-layouts: 1.14 us -> none  [per_device(): jnp.pad(expansion_basis.T, ((0, ROWS - expansion_basis.shape[1]), (0, 0)))]
    reshape x1 -> x0, local copies, waits for them, and re-layouts: 0.9 us -> none  [per_device(): own = own.reshape(ROWS, CHUNKS, KC).swapaxes(0, 1)]
where the time goes in v3:
time: 79.8 us; the launch traced here: 79.7 us
  Pallas kernels  77.9 us (98%)
  local copies, waits for them, and re-layouts  1.08 us (1%)
    pallas_call x1, Pallas kernels, per_device(): pl.pallas_call(functools.partial(gather_dot, plan), out_shape=jax.ShapeDt...  51.4 us
    pallas_call x1, Pallas kernels, per_device(): pl.pallas_call(functools.partial(reduce_iterate, scale), out_shape=jax.Sh...  22.7 us
    pallas_call x1, Pallas kernels, per_device(): pl.pallas_call(cut_windows, out_shape=(jax.ShapeDtypeStruct((4, 2, *tiles...  1.92 us
    pallas_call x1, Pallas kernels, per_device(): pl.pallas_call(project, out_shape=(jax.ShapeDtypeStruct((rows, 2 * L * KM...  1.87 us

profile of v3, /device:TPU:1, one launch (start us, length us, event | category | flops | bytes accessed | tf_op | source)
XLA Modules:
  0.0 79.7 jit_solution(5010069863778158458)
XLA Ops:
  0.6 0.0 copy-start.2
  0.6 0.0 copy-start.3
  0.7 0.0 copy-start
  0.7 1.1 %copy-done = bf16[9216,30]{0,1:T(8,128)(2,1)S(1)} copy-done((bf16[9216,30]{0,1:T(8,128)(2,1)S(1)}, bf16[9216,30]{0,1:T(8,128)(2,1)}, u32[]{:S(2)}) %copy-start) | copy-done | bytes 552984
  1.7 0.0 copy-start.1
  1.7 51.4 %shard_map.68.coeffs = bf16[384,1024]{1,0:T(8,128)(2,1)S(1)} custom-call(bf16[384,9216]{1,0:T(8,128)(2,1)} %images.1, bf16[30,9216]{1,0:T(8,128)(2,1)S(1)} %bitcast.3), custom_call_target="tpu_custom_call" | custom-call | tf_op jit(solution)/shard_map/pallas_call | solution.py:379
  53.1 0.0 copy-done.2
  53.1 0.0 copy-done.3
  53.2 0.0 copy-done.1
  53.2 1.9 %shard_map.69 = (f32[4,2,3,32,128]{4,3,2,1,0:T(8,128)S(1)}, f32[3,128,128]{2,1,0:T(8,128)S(1)}) custom-call(s32[16]{0:T(128)S(1)} %copy-done.2, s32[16]{0:T(128)S(1)} %copy-done.3, bf16[384,1024]{1,0:T(8,128)(2,1)S(1)} %shard_map.68.coeffs, f32[16,8,80]{2,1,0:T(8,128)S(1)} %bitcast.4), custom_call_target="tpu_custom_call" | custom-call | tf_op jit(solution)/shard_map/pallas_call | solution.py:396
  55.1 22.7 %shard_map.70.everything = f32[128,128]{1,0:T(8,128)S(1)} custom-call(f32[4,2,3,32,128]{4,3,2,1,0:T(8,128)S(1)} %get-tuple-element.6.packed, f32[3,128,128]{2,1,0:T(8,128)S(1)} %get-tuple-element.7.begin), custom_call_target="tpu_custom_call" | custom-call | tf_op jit(solution)/shard_map/pallas_call | solution.py:404
  77.8 1.9 %shard_map.71 = (f32[384,256]{1,0:T(8,128)}, f32[8,16]{1,0:T(8,128)}) custom-call(s32[16]{0:T(128)S(1)} %copy-done.2, bf16[384,1024]{1,0:T(8,128)(2,1)S(1)} %shard_map.68.coeffs, f32[128,128]{1,0:T(8,128)S(1)} %shard_map.70.everything), custom_call_target="tpu_custom_call" | custom-call | tf_op jit(solution)/shard_map/pallas_call | solution.py:424
Async XLA Ops:
  0.6 52.5 %copy-start.2 = (s32[16]{0:T(128)S(1)}, s32[16]{0:T(128)}, u32[]{:S(2)}) copy-start(s32[16]{0:T(128)} %sizes.3) | copy-start | bytes 196
  0.6 52.5 %copy-start.3 = (s32[16]{0:T(128)S(1)}, s32[16]{0:T(128)}, u32[]{:S(2)}) copy-start(s32[16]{0:T(128)} %keeps.1) | copy-start | bytes 196
  0.7 1.1 %copy-start = (bf16[9216,30]{0,1:T(8,128)(2,1)S(1)}, bf16[9216,30]{0,1:T(8,128)(2,1)}, u32[]{:S(2)}) copy-start(bf16[9216,30]{0,1:T(8,128)(2,1)} %param.6) | copy-start | bytes 1658884
  1.7 51.4 %copy-start.1 = (f32[16,80,8]{1,2,0:T(8,128)S(1)}, f32[16,80,8]{1,2,0:T(8,128)}, u32[]{:S(2)}) copy-start(f32[16,80,8]{1,2,0:T(8,128)} %param.9) | copy-start | bytes 122884

commit v4 on v3

--- a/solution.py
+++ b/solution.py
@@ -25,13 +25,14 @@
 CHUNKS = 36
 ROWS = 32
 BLOCK = ROWS * KC * 2
+PLANE = (-1, 1, -1, 1)
 PART = 16 * ROWS
 WIN = 96
 
 
 class Plan:
     def __init__(
-        self, window=2.5, late=0.3, turns=0.5, rate=42.5e3, hop=2.8, d_rate=600e3, d_hop=1.4, dot=0.25, queue=3
+        self, window=2.5, late=0.3, turns=0.5, spare=-1.0, rate=42.5e3, hop=2.8, d_rate=600e3, d_hop=1.4, dot=0.25, queue=3
     ):
         self.program = []
         self.sems = {}
@@ -62,6 +63,9 @@
                 while line and busy.get(link, 0.0) < self.now + window:
                     _, _, key, size = heapq.heappop(line)
                     issue(key, link, size)
+
+        def enqueue(link, rank, key):
+            heapq.heappush(pending.setdefault(link, []), (rank, next(count), key, SIZES[key[0]] * BLOCK))
 
         def along(axis, place, at, key):
             forward = -1 if key[1] % 2 == 0 else 1
@@ -73,9 +77,7 @@
                 steps = ()
             for there, sign in steps:
                 onto = key[:at] + (there,) + key[at + 1 :]
-                rank = onto[0] * late + onto[1] * turns - to_go(onto)
-                line = pending.setdefault(axis + sign, [])
-                heapq.heappush(line, (rank, next(count), onto, SIZES[key[0]] * BLOCK))
+                enqueue(axis + sign, onto[0] * late + onto[1] * turns - to_go(onto), onto)
 
         def onward(key):
             r, sub, da, db, dx = key
@@ -84,7 +86,7 @@
                 if db == 0:
                     along(first, da, 2, key)
                 along(second, db, 3, key)
-            if r == 0 and (da, db) != (0, 0):
+            if r == 0 and (da, db) not in ((0, 0), (PLANE[sub], 0)):
                 along("x", dx, 4, key)
 
         def got(group, need):
@@ -94,6 +96,11 @@
         for r in range(len(SIZES)):
             for sub in range(SUBS):
                 onward((r, sub, 0, 0, 0))
+        for sub in range(SUBS):
+            for dx in (-1, 1, 2):
+                if PLANE[sub]:
+                    link = ("y" if sub < 2 else "z") + ("+" if PLANE[sub] < 0 else "-")
+                    enqueue(link, spare + sub * turns, (0, sub, PLANE[sub], 0, dx))
         pump()
         while heap or ready:
             if ready and (not heap or heap[0][0] > self.now or len(ready) > queue):
@@ -126,18 +133,21 @@
     return tuple(spot[a] for a in "yzcx")
 
 
-def gather_dot(plan, images, basis, coeffs, held, pixels, total, fill_sem, send_sem, recv_sem):
+def gather_dot(plan, images, basis, coeffs, held, stage, pixels, total, fill_sem, send_sem, recv_sem):
     y, z, c, x = (lax.axis_index(a) for a in AXES)
     sibling = (y, z, 1 - c, x)
     barrier = pltpu.get_barrier_semaphore()
+    own = pltpu.make_async_copy(basis, stage, fill_sem.at[0])
+    own.start()
     for peer in [device(axis, by) for axis in "yzx" for by in (1, -1)] + [sibling]:
         pl.semaphore_signal(barrier, inc=1, device_id=peer, device_id_type=MESH)
-    fill = pltpu.make_async_copy(images, pixels, fill_sem)
+    total[...] = jnp.zeros_like(total)
+    own.wait()
+    fill = pltpu.make_async_copy(images, pixels, fill_sem.at[1])
     fill.start()
     for k in range(CHUNKS):
         held[k, y, z, c] = jnp.zeros((ROWS, KC), jnp.bfloat16)
-        held[k, y, z, c, : basis.shape[0]] = basis[:, k * KC : (k + 1) * KC]
-    total[...] = jnp.zeros_like(total)
+        held[k, y, z, c, : stage.shape[0]] = stage[:, k * KC : (k + 1) * KC]
     pl.semaphore_wait(barrier, 7)
 
     def index(r, sub, dx):
@@ -154,7 +164,7 @@
         else:
             r, sub = key[:2]
             place = list(key[2:])
-            moving = 2 if place[2] else 1 if place[1] else 0
+            moving = 2 if place[2] and place[:2] != [PLANE[sub], 0] else 1 if place[1] else 0
             forward = -1 if sub % 2 == 0 else 1
             there = place[moving]
             step = -there if there != 2 else -forward
@@ -379,20 +389,21 @@
     coeffs = pl.pallas_call(
         functools.partial(gather_dot, plan),
         out_shape=jax.ShapeDtypeStruct((rows, 2 * PART), bf16),
-        in_specs=[pl.BlockSpec(memory_space=pltpu.HBM), vmem],
+        in_specs=[pl.BlockSpec(memory_space=pltpu.HBM)] * 2,
         out_specs=vmem,
         scratch_shapes=[
             pltpu.VMEM((CHUNKS, 4, 4, 2, ROWS, KC), bf16),
+            pltpu.VMEM((expansion_basis.shape[1], expansion_basis.shape[0]), bf16),
             pltpu.VMEM(images.shape, bf16),
             pltpu.VMEM((rows, 2 * PART), f32),
-            pltpu.SemaphoreType.DMA,
+            pltpu.SemaphoreType.DMA((2,)),
             pltpu.SemaphoreType.DMA,
             pltpu.SemaphoreType.DMA((len(plan.sems),)),
         ],
         compiler_params=pltpu.CompilerParams(
             collective_id=0, has_side_effects=True, vmem_limit_bytes=52 * 1024 * 1024
         ),
-    )(images, expansion_basis.T)
+    )(images, pltpu.with_memory_space_constraint(expansion_basis.T, pltpu.HBM))
     packed, begin = pl.pallas_call(
         cut_windows,
         out_shape=(jax.ShapeDtypeStruct((4, 2, *tiles), f32), jax.ShapeDtypeStruct((3, L * KMAX, 128), f32)),

time: 79.8 us -> 78 us (0.977)
  local copies, waits for them, and re-layouts: 1.08 us -> 0.01 us
  Pallas kernels: 77.9 us -> 77.1 us
    unnamed x8 -> x6, local copies, waits for them, and re-layouts: 1.08 us -> 0.01 us
where the time goes in v4:
time: 78 us; the launch traced here: 77.8 us
  Pallas kernels  77.1 us (99%)
    pallas_call x1, Pallas kernels, per_device(): pl.pallas_call(functools.partial(gather_dot, plan), out_shape=jax.ShapeDt...  50.9 us
    pallas_call x1, Pallas kernels, per_device(): pl.pallas_call(functools.partial(reduce_iterate, scale), out_shape=jax.Sh...  22.4 us
    pallas_call x1, Pallas kernels, per_device(): pl.pallas_call(cut_windows, out_shape=(jax.ShapeDtypeStruct((4, 2, *tiles...  1.93 us
    pallas_call x1, Pallas kernels, per_device(): pl.pallas_call(project, out_shape=(jax.ShapeDtypeStruct((rows, 2 * L * KM...  1.87 us

profile of v4, /device:TPU:1, one launch (start us, length us, event | category | flops | bytes accessed | tf_op | source)
XLA Modules:
  0.0 77.8 jit_solution(3119037858787169476)
XLA Ops:
  0.6 0.0 copy-start.1
  0.6 0.0 copy-start
  0.7 0.0 copy-start.2
  0.7 50.9 %shard_map.68.coeffs = bf16[384,1024]{1,0:T(8,128)(2,1)S(1)} custom-call(bf16[384,9216]{1,0:T(8,128)(2,1)} %images.1, bf16[30,9216]{1,0:T(8,128)(2,1)} %bitcast.4), custom_call_target="tpu_custom_call" | custom-call | tf_op jit(solution)/shard_map/pallas_call | solution.py:389
  51.6 0.0 copy-done.1
  51.6 0.0 copy-done
  51.6 0.0 copy-done.2
  51.6 1.9 %shard_map.69 = (f32[4,2,3,32,128]{4,3,2,1,0:T(8,128)S(1)}, f32[3,128,128]{2,1,0:T(8,128)S(1)}) custom-call(s32[16]{0:T(128)S(1)} %copy-done.1, s32[16]{0:T(128)S(1)} %copy-done.2, bf16[384,1024]{1,0:T(8,128)(2,1)S(1)} %shard_map.68.coeffs, f32[16,8,80]{2,1,0:T(8,128)S(1)} %bitcast.3), custom_call_target="tpu_custom_call" | custom-call | tf_op jit(solution)/shard_map/pallas_call | solution.py:407
  53.6 22.4 %shard_map.70.everything = f32[128,128]{1,0:T(8,128)S(1)} custom-call(f32[4,2,3,32,128]{4,3,2,1,0:T(8,128)S(1)} %get-tuple-element.6.packed, f32[3,128,128]{2,1,0:T(8,128)S(1)} %get-tuple-element.7.begin), custom_call_target="tpu_custom_call" | custom-call | tf_op jit(solution)/shard_map/pallas_call | solution.py:415
  76.0 1.9 %shard_map.71 = (f32[384,256]{1,0:T(8,128)}, f32[8,16]{1,0:T(8,128)}) custom-call(s32[16]{0:T(128)S(1)} %copy-done.1, bf16[384,1024]{1,0:T(8,128)(2,1)S(1)} %shard_map.68.coeffs, f32[128,128]{1,0:T(8,128)S(1)} %shard_map.70.everything), custom_call_target="tpu_custom_call" | custom-call | tf_op jit(solution)/shard_map/pallas_call | solution.py:435
Async XLA Ops:
  0.6 51.0 %copy-start.1 = (s32[16]{0:T(128)S(1)}, s32[16]{0:T(128)}, u32[]{:S(2)}) copy-start(s32[16]{0:T(128)} %sizes.3) | copy-start | bytes 196
  0.6 51.0 %copy-start = (f32[16,80,8]{1,2,0:T(8,128)S(1)}, f32[16,80,8]{1,2,0:T(8,128)}, u32[]{:S(2)}) copy-start(f32[16,80,8]{1,2,0:T(8,128)} %param.9) | copy-start | bytes 122884
  0.7 51.0 %copy-start.2 = (s32[16]{0:T(128)S(1)}, s32[16]{0:T(128)}, u32[]{:S(2)}) copy-start(s32[16]{0:T(128)} %keeps.1) | copy-start | bytes 196

commit v5 on v4

--- a/solution.py
+++ b/solution.py
@@ -26,6 +26,7 @@
 ROWS = 32
 BLOCK = ROWS * KC * 2
 PLANE = (-1, 1, -1, 1)
+FIRST_FAR = (2, 1, 3)
 PART = 16 * ROWS
 WIN = 96
 
@@ -322,7 +323,7 @@
         for xo in range(4):
             half[h, xo] = packed[xo, c, :, lines] + mate[xo, :, lines]
         copies.append([
-            push(half.at[h, turn(x, by)], by_x.at[h, by - 1], far(0, h)[by - 1], device("x", by)) for by in (1, 2, 3)
+            push(half.at[h, turn(x, by)], by_x.at[h, by - 1], far(0, h)[by - 1], device("x", by)) for by in FIRST_FAR
         ])
     for stage, (land, spots, axes) in enumerate(((one, (y, z), "yz"), (two, (z, y), "zy"))):
         onward = []
@@ -336,7 +337,7 @@
                 land[h, spot] = one[h, 0] + one[h, 1] + one[h, 2] + one[h, 3]
             onward.append([
                 push(land.at[h, spot], land.at[h, spot], far(1 + stage, h)[by - 1], device(axes[h], by))
-                for by in (1, 2, 3)
+                for by in FIRST_FAR
             ])
         copies = onward
     for h in range(2):
@@ -348,7 +349,7 @@
     me = 2 * x + c
     lines = pl.ds(pl.multiple_of(2 * KMAX * me, 2 * KMAX), 2 * KMAX)
     found[me] = iterate(summed, begin[0, lines], begin[1, lines], begin[2, lines])
-    copies = [push(found.at[me], found.at[me], (found_sem.at[0, e], found_sem.at[1, e]), owners[e]) for e in range(7)]
+    copies = [push(found.at[me], found.at[me], (found_sem.at[0, e], found_sem.at[1, e]), owners[e]) for e in (1, 5, 0, 2, 4, 6, 3)]
     for copy in copies:
         copy.wait_recv()
     everything[...] = found[...].reshape(L * KMAX, 128)

time: 78 us -> 77.5 us (level)
  no operation moved by 1% of the time
where the time goes in v5:
time: 77.5 us; the launch traced here: 77.4 us
  Pallas kernels  76.7 us (99%)
    pallas_call x1, Pallas kernels, per_device(): pl.pallas_call(functools.partial(gather_dot, plan), out_shape=jax.ShapeDt...  50.9 us
    pallas_call x1, Pallas kernels, per_device(): pl.pallas_call(functools.partial(reduce_iterate, scale), out_shape=jax.Sh...  22 us
    pallas_call x1, Pallas kernels, per_device(): pl.pallas_call(cut_windows, out_shape=(jax.ShapeDtypeStruct((4, 2, *tiles...  1.92 us
    pallas_call x1, Pallas kernels, per_device(): pl.pallas_call(project, out_shape=(jax.ShapeDtypeStruct((rows, 2 * L * KM...  1.87 us

profile of v5, /device:TPU:1, one launch (start us, length us, event | category | flops | bytes accessed | tf_op | source)
XLA Modules:
  0.0 77.4 jit_solution(6797531502727732799)
XLA Ops:
  0.6 0.0 copy-start.1
  0.6 0.0 copy-start
  0.7 0.0 copy-start.2
  0.7 50.9 %shard_map.68.coeffs = bf16[384,1024]{1,0:T(8,128)(2,1)S(1)} custom-call(bf16[384,9216]{1,0:T(8,128)(2,1)} %images.1, bf16[30,9216]{1,0:T(8,128)(2,1)} %bitcast.4), custom_call_target="tpu_custom_call" | custom-call | tf_op jit(solution)/shard_map/pallas_call | solution.py:390
  51.6 0.0 copy-done.1
  51.6 0.0 copy-done
  51.6 0.0 copy-done.2
  51.6 1.9 %shard_map.69 = (f32[4,2,3,32,128]{4,3,2,1,0:T(8,128)S(1)}, f32[3,128,128]{2,1,0:T(8,128)S(1)}) custom-call(s32[16]{0:T(128)S(1)} %copy-done.1, s32[16]{0:T(128)S(1)} %copy-done.2, bf16[384,1024]{1,0:T(8,128)(2,1)S(1)} %shard_map.68.coeffs, f32[16,8,80]{2,1,0:T(8,128)S(1)} %bitcast.3), custom_call_target="tpu_custom_call" | custom-call | tf_op jit(solution)/shard_map/pallas_call | solution.py:408
  53.6 22.0 %shard_map.70.everything = f32[128,128]{1,0:T(8,128)S(1)} custom-call(f32[4,2,3,32,128]{4,3,2,1,0:T(8,128)S(1)} %get-tuple-element.6.packed, f32[3,128,128]{2,1,0:T(8,128)S(1)} %get-tuple-element.7.begin), custom_call_target="tpu_custom_call" | custom-call | tf_op jit(solution)/shard_map/pallas_call | solution.py:416
  75.6 1.9 %shard_map.71 = (f32[384,256]{1,0:T(8,128)}, f32[8,16]{1,0:T(8,128)}) custom-call(s32[16]{0:T(128)S(1)} %copy-done.1, bf16[384,1024]{1,0:T(8,128)(2,1)S(1)} %shard_map.68.coeffs, f32[128,128]{1,0:T(8,128)S(1)} %shard_map.70.everything), custom_call_target="tpu_custom_call" | custom-call | tf_op jit(solution)/shard_map/pallas_call | solution.py:436
Async XLA Ops:
  0.6 51.0 %copy-start.1 = (s32[16]{0:T(128)S(1)}, s32[16]{0:T(128)}, u32[]{:S(2)}) copy-start(s32[16]{0:T(128)} %sizes.3) | copy-start | bytes 196
  0.6 51.0 %copy-start = (f32[16,80,8]{1,2,0:T(8,128)S(1)}, f32[16,80,8]{1,2,0:T(8,128)}, u32[]{:S(2)}) copy-start(f32[16,80,8]{1,2,0:T(8,128)} %param.9) | copy-start | bytes 122884
  0.7 51.0 %copy-start.2 = (s32[16]{0:T(128)S(1)}, s32[16]{0:T(128)}, u32[]{:S(2)}) copy-start(s32[16]{0:T(128)} %keeps.1) | copy-start | bytes 196
